TPU v7x, 32 devices: a whole 2x2x4 slice. The times are simulated.
32 devices in a mesh: gy: 8 (over z, x), gx: 4 (over y, core).
Axes of the slice: x: 2, y: 2, z: 4, core: 2. Of those that a mesh axis runs over, the one named last changes fastest.
Arguments:
- ensemble: bfloat16 [32, 2, 512, 512], P(None, None, 'gy', 'gx'), may hold values from -1.1953125 to 1.1953125
- obs_cell: int32 [8, 4, 2048], P('gy', 'gx'), may hold values from 0 to 8191
- obs_level: int32 [8, 4, 2048], P('gy', 'gx'), may hold values from 0 to 1
- innovation: float32 [8, 4, 2048], P('gy', 'gx'), may hold values from -6 to 6
- obs_weight: float32 [8, 4, 2048], P('gy', 'gx'), may hold values from 0.5 to 4
Outputs:
- control: float32 [32, 2, 512, 512], P(None, None, 'gy', 'gx')
- increment: float32 [2, 512, 512], P(None, 'gy', 'gx')
Inputs may be any that keep to these rules, and one draw needn't show every extreme that they name: obs_cell holds row * 128 + column of the observation within its device's block of 64 x 128 cells.
All inputs are finite; a program needn't handle non-finite values.
Results may differ from a plain program's by a relative error of at most 0.0003.
Values sent between devices are 32-bit elements; how exact they have to be, the bound alone decides.
A program may use at most 128 MiB of HBM per device.

v0:
```python
import jax
import jax.numpy as jnp
from jax import lax
from jax.sharding import PartitionSpec as P

SWEEPS = 4


KAPPA = 0.2
EPS = 1e-06


def with_halo(cells, sides, width):
    for axis, dim in sides:
        count = lax.axis_size(axis)
        ends = count - 1
        head = lax.slice_in_dim(cells, 0, width, axis=dim)
        tail = lax.slice_in_dim(cells, cells.shape[dim] - width, cells.shape[dim], axis=dim)
        cells = jnp.concatenate(
            [
                lax.ppermute(tail, axis, [(i, (i + 1) % count) for i in range(ends)]),
                cells,
                lax.ppermute(head, axis, [((i + 1) % count, i) for i in range(ends)]),
            ],
            axis=dim,
        )
    return cells


def filtered(field):
    rows = field.shape[2]
    cols = field.shape[3]
    padded = with_halo(field, (("gy", 2), ("gx", 3)), SWEEPS)
    row_pos = lax.axis_index("gy") * rows - SWEEPS + jnp.arange(rows + 2 * SWEEPS, dtype=jnp.int32)
    col_pos = lax.axis_index("gx") * cols - SWEEPS + jnp.arange(cols + 2 * SWEEPS, dtype=jnp.int32)
    row_mask = ((row_pos >= 0) & (row_pos < rows * lax.axis_size("gy"))).astype(jnp.float32)
    col_mask = ((col_pos >= 0) & (col_pos < cols * lax.axis_size("gx"))).astype(jnp.float32)
    for sweep in range(1, SWEEPS + 1):
        inner = padded[:, :, 1:-1, 1:-1]
        beside_all = (
            padded[:, :, 2:, 1:-1]
            + padded[:, :, :-2, 1:-1]
            + padded[:, :, 1:-1, 2:]
            + padded[:, :, 1:-1, :-2]
        )
        padded = inner + KAPPA * (beside_all - 4.0 * inner)
        row_keep = row_mask[sweep : rows + 2 * SWEEPS - sweep]
        col_keep = col_mask[sweep : cols + 2 * SWEEPS - sweep]
        padded = padded * (row_keep[:, None] * col_keep[None, :])
    return padded


def on_device(ensemble, obs_cell, obs_level, innovation, obs_weight):
    levels = ensemble.shape[1]
    rows = ensemble.shape[2]
    cols = ensemble.shape[3]
    points = (obs_level * (rows * cols) + obs_cell).reshape(-1)
    weights = obs_weight.reshape(-1)

    def adjoint_obs(values):
        state = jnp.zeros((levels * rows * cols,), jnp.float32).at[points].add(values)
        return state.reshape(levels, rows, cols)

    def hessian(vector):
        state = jnp.sum(ensemble * filtered(vector), axis=0)
        seen = state.reshape(-1)[points]
        back = filtered(ensemble * adjoint_obs(weights * seen)[None])
        return (vector + back, state)

    gradient = filtered(ensemble * adjoint_obs(weights * innovation.reshape(-1))[None])
    bnorm = jnp.sqrt(lax.psum(jnp.sum(gradient * gradient), ("gy", "gx")) + EPS)
    first = gradient / bnorm
    image_one, state_one = hessian(first)
    alpha_one = lax.psum(jnp.sum(first * image_one), ("gy", "gx"))
    remain = image_one - alpha_one * first
    beta_sq = lax.psum(jnp.sum(remain * remain), ("gy", "gx"))
    beta = jnp.sqrt(beta_sq + EPS)
    second = remain / beta
    image_two, state_two = hessian(second)
    alpha_two = lax.psum(jnp.sum(second * image_two), ("gy", "gx"))
    determ = alpha_one * alpha_two - beta * beta
    coef_one = bnorm * alpha_two / determ
    coef_two = -bnorm * beta / determ
    control = coef_one * first + coef_two * second
    increment = coef_one * state_one + coef_two * state_two
    return (control, increment)


def solution(mesh):
    return jax.shard_map(
        on_device,
        mesh=mesh,
        in_specs=(
            P(None, None, "gy", "gx"),
            P("gy", "gx", None),
            P("gy", "gx", None),
            P("gy", "gx", None),
            P("gy", "gx", None),
        ),
        out_specs=(P(None, None, "gy", "gx"), P(None, "gy", "gx")),
        check_vma=False,
    )
```

profile of v0, /device:TPU:0, one launch (start us, length us, event | category | flops | bytes accessed | tf_op | source)
XLA Modules:
  0.0 534.0 jit_solution(15424019485142856667)
XLA Ops:
  2.1 11.3 %scatter_custom_fusion = f32[16384]{0:T(1024)S(1)} fusion(s32[2048]{0:T(1024)S(1)} %bitcast.18, f32[2048]{0:T(1024)S(1)} %mul.242, f32[]{:T(128)} %constant.14.clone.1), kind=kCustom, calls=%fused_computation.181 | custom fusion | flops 2048 | bytes 65540 | tf_op jit(solution)/shard_map/scatter-add | solution.py:61
  15.3 4.9 collective-permute-start
  22.9 4.1 collective-permute-done.1
  45.4 5.0 pad_maximum_fusion
  50.4 5.0 fusion.19
  55.4 4.8 fusion.39
  60.2 4.7 fusion.59
  67.7 44.1 %psum.28 = f32[]{:T(128)} all-reduce(f32[]{:T(128)} %get-tuple-element.12), channel_id=1, replica_groups=mesh['gy'=8,'gx'=4] {'gy','gx'}, use_global_device_ids=true, to_apply=%region_2.0 | all-reduce | flops 1 | bytes 8 | tf_op jit(solution)/shard_map/psum | solution.py:71
  112.8 4.2 collective-permute-start.4
  141.7 4.8 pad_maximum_fusion.1
  146.5 5.0 fusion.15
  151.5 4.8 fusion.35
  156.3 4.7 fusion.55
  163.3 11.8 %gather_fusion = f32[2048]{0:T(1024)S(1)} fusion(f32[16384]{0:T(1024)S(1)} %bitcast.10, s32[2048]{0:T(1024)S(1)} %broadcast_clamp_fusion), kind=kCustom, calls=%fused_computation | custom fusion | bytes 24576 | tf_op jit(solution)/shard_map/gather | solution.py:66
  175.7 11.8 %scatter_custom_fusion.1 = f32[16384]{0:T(1024)S(1)} fusion(s32[2048]{0:T(1024)S(1)} %bitcast.20, f32[2048]{0:T(1024)} %mul.290, f32[]{:T(128)} %constant.14.clone.1), kind=kCustom, calls=%fused_computation.179 | custom fusion | flops 2048 | bytes 66048 | tf_op jit(solution)/shard_map/scatter-add | solution.py:61
  188.3 3.7 collective-permute-start.8
  194.5 4.4 collective-permute-done.9
  202.7 3.5 copy.50
  206.2 4.7 collective-permute-start.10
  215.6 4.1 copy.52
  219.7 4.1 copy.53
  223.8 4.9 pad_maximum_fusion.2
  228.7 5.0 fusion.11
  233.6 4.8 fusion.31
  238.4 4.7 fusion.51
  243.1 4.0 multiply_reduce_fusion.1
  247.1 42.5 %psum.29 = f32[]{:T(128)} all-reduce(f32[]{:T(128)} %get-tuple-element.10), channel_id=1, replica_groups=mesh['gy'=8,'gx'=4] {'gy','gx'}, use_global_device_ids=true, to_apply=%region_6.0 | all-reduce | flops 1 | bytes 8 | tf_op jit(solution)/shard_map/psum | solution.py:74
  293.0 39.4 %psum.30 = f32[]{:T(128)} all-reduce(f32[]{:T(128)} %multiply_reduce_fusion), channel_id=1, replica_groups=mesh['gy'=8,'gx'=4] {'gy','gx'}, use_global_device_ids=true, to_apply=%region_8.0 | all-reduce | flops 1 | bytes 8 | tf_op jit(solution)/shard_map/psum | solution.py:76
  335.9 4.2 collective-permute-start.12
  342.6 4.4 collective-permute-done.13
  350.8 3.5 copy.54
  361.0 4.1 copy.56
  365.1 4.1 copy.57
  369.2 5.1 pad_maximum_fusion.3
  374.2 5.0 fusion.7
  379.2 4.8 fusion.27
  384.0 4.7 fusion.47
  391.0 20.6 %gather_fusion.1 = f32[2048]{0:T(1024)} fusion(f32[16384]{0:T(1024)S(1)} %bitcast.11, s32[2048]{0:T(1024)S(1)} %broadcast_clamp_fusion), kind=kCustom, calls=%fused_computation.1 | custom fusion | bytes 24576 | tf_op jit(solution)/shard_map/gather | solution.py:66
  412.2 12.2 %scatter_custom_fusion.2 = f32[16384]{0:T(1024)} fusion(s32[2048]{0:T(1024)S(1)} %bitcast.21, f32[2048]{0:T(1024)S(1)} %mul.630, f32[]{:T(128)} %constant.14.clone.1), kind=kCustom, calls=%fused_computation.177 | custom fusion | flops 2048 | bytes 65540 | tf_op jit(solution)/shard_map/scatter-add | solution.py:61
  426.0 4.0 collective-permute-start.16
  432.5 4.4 collective-permute-done.17
  442.9 4.0 collective-permute-start.18
  458.3 5.0 pad_maximum_fusion.4
  463.3 5.0 fusion.3
  468.2 4.8 fusion.23
  473.0 4.7 fusion.43
  480.7 42.8 %psum.31 = f32[]{:T(128)} all-reduce(f32[]{:T(128)} %fusion.60), channel_id=1, replica_groups=mesh['gy'=8,'gx'=4] {'gy','gx'}, use_global_device_ids=true, to_apply=%region_12.0 | all-reduce | flops 1 | bytes 8 | tf_op jit(solution)/shard_map/psum | solution.py:80
  529.6 4.1 copy.64
  (114 shorter events, 117.4 us)
Async XLA Ops:
  15.3 7.6 %collective-permute-start = (f32[32,2,4,128]{3,0,2,1:T(8,128)S(1)}, f32[32,2,4,128]{3,0,2,1:T(8,128)S(1)}, u32[]{:S(2)}, u32[]{:S(2)}) collective-permute-start(f32[32,2,4,128]{3,0,2,1:T(8,128)S(1)} %get-tuple-element.32), channel_id=1, source_target_pairs={{0,4},{4,8},{8,12},{12,16},{16,20},{20,24},{24,28},{1,5},{5,9},{9,... | collective-permute-start | bytes 393224 | tf_op jit(solution)/shard_map/ppermute | solution.py:21
  20.2 6.9 %collective-permute-start.1 = (f32[32,2,4,128]{3,0,2,1:T(8,128)S(1)}, f32[32,2,4,128]{3,0,2,1:T(8,128)S(1)}, u32[]{:S(2)}, u32[]{:S(2)}) collective-permute-start(f32[32,2,4,128]{3,0,2,1:T(8,128)S(1)} %get-tuple-element.33), channel_id=1, source_target_pairs={{4,0},{8,4},{12,8},{16,12},{20,16},{24,20},{28,24},{5,1},{9,5},{13... | collective-permute-start | bytes 393224 | tf_op jit(solution)/shard_map/ppermute | solution.py:23
  33.1 5.5 %collective-permute-start.2 = (f32[32,2,72,4]{2,0,3,1:T(8,128)S(1)}, f32[32,2,72,4]{2,0,3,1:T(8,128)S(1)}, u32[]{:S(2)}, u32[]{:S(2)}) collective-permute-start(f32[32,2,72,4]{2,0,3,1:T(8,128)S(1)} %copy.40), channel_id=1, source_target_pairs={{0,1},{1,2},{2,3},{4,5},{5,6},{6,7},{8,9},{9,10},{10,11},{12,13},{... | collective-permute-start | bytes 221192 | tf_op jit(solution)/shard_map/ppermute | solution.py:21
  37.2 5.0 collective-permute-start.3
  112.7 11.1 %copy-start.4 = (f32[32,2,64,128]{3,0,2,1:T(8,128)}, f32[32,2,64,128]{3,0,2,1:T(8,128)S(1)}, u32[]{:S(2)}) copy-start(f32[32,2,64,128]{3,0,2,1:T(8,128)S(1)} %broadcast_divide_fusion.1) | copy-start | bytes 6291460
  112.8 8.1 %collective-permute-start.4 = (f32[32,2,4,128]{3,0,2,1:T(8,128)S(1)}, f32[32,2,4,128]{3,0,2,1:T(8,128)S(1)}, u32[]{:S(2)}, u32[]{:S(2)}) collective-permute-start(f32[32,2,4,128]{3,0,2,1:T(8,128)S(1)} %get-tuple-element.30), channel_id=1, source_target_pairs={{0,4},{4,8},{8,12},{12,16},{16,20},{20,24},{24,28},{1,5},{5,9},{9,... | collective-permute-start | bytes 393224 | tf_op jit(solution)/shard_map/ppermute | solution.py:21
  117.0 6.9 %collective-permute-start.5 = (f32[32,2,4,128]{3,0,2,1:T(8,128)S(1)}, f32[32,2,4,128]{3,0,2,1:T(8,128)S(1)}, u32[]{:S(2)}, u32[]{:S(2)}) collective-permute-start(f32[32,2,4,128]{3,0,2,1:T(8,128)S(1)} %get-tuple-element.31), channel_id=1, source_target_pairs={{4,0},{8,4},{12,8},{16,12},{20,16},{24,20},{28,24},{5,1},{9,5},{13... | collective-permute-start | bytes 393224 | tf_op jit(solution)/shard_map/ppermute | solution.py:23
  129.9 5.4 %collective-permute-start.6 = (f32[32,2,72,4]{2,0,3,1:T(8,128)S(1)}, f32[32,2,72,4]{2,0,3,1:T(8,128)S(1)}, u32[]{:S(2)}, u32[]{:S(2)}) collective-permute-start(f32[32,2,72,4]{2,0,3,1:T(8,128)S(1)} %copy.44), channel_id=1, source_target_pairs={{0,1},{1,2},{2,3},{4,5},{5,6},{6,7},{8,9},{9,10},{10,11},{12,13},{... | collective-permute-start | bytes 221192 | tf_op jit(solution)/shard_map/ppermute | solution.py:21
  134.0 4.5 collective-permute-start.7
  156.3 4.7 copy-start.2
  163.2 11.8 %copy-start.10 = (f32[1,1,2048]{2,1,0:T(1,128)S(1)}, f32[1,1,2048]{2,1,0:T(1,128)}, u32[]{:S(2)}) copy-start(f32[1,1,2048]{2,1,0:T(1,128)} %param.9) | copy-start | bytes 24580
  188.2 10.6 %copy-start.5 = (f32[32,2,64,128]{3,0,2,1:T(8,128)}, f32[32,2,64,128]{3,0,2,1:T(8,128)S(1)}, u32[]{:S(2)}) copy-start(f32[32,2,64,128]{3,0,2,1:T(8,128)S(1)} %convert_multiply_fusion.2) | copy-start | bytes 6291460
  188.3 6.2 %collective-permute-start.8 = (f32[32,2,4,128]{3,0,2,1:T(8,128)S(1)}, f32[32,2,4,128]{3,0,2,1:T(8,128)S(1)}, u32[]{:S(2)}, u32[]{:S(2)}) collective-permute-start(f32[32,2,4,128]{3,0,2,1:T(8,128)S(1)} %get-tuple-element.28), channel_id=1, source_target_pairs={{0,4},{4,8},{8,12},{12,16},{16,20},{20,24},{24,28},{1,5},{5,9},{9,... | collective-permute-start | bytes 393224 | tf_op jit(solution)/shard_map/ppermute | solution.py:21
  192.0 6.9 %collective-permute-start.9 = (f32[32,2,4,128]{3,0,2,1:T(8,128)S(1)}, f32[32,2,4,128]{3,0,2,1:T(8,128)S(1)}, u32[]{:S(2)}, u32[]{:S(2)}) collective-permute-start(f32[32,2,4,128]{3,0,2,1:T(8,128)S(1)} %get-tuple-element.29), channel_id=1, source_target_pairs={{4,0},{8,4},{12,8},{16,12},{20,16},{24,20},{28,24},{5,1},{9,5},{13... | collective-permute-start | bytes 393224 | tf_op jit(solution)/shard_map/ppermute | solution.py:23
  194.5 4.4 copy-start.6
  198.8 0.6 copy-start.8
  206.2 9.4 %collective-permute-start.10 = (f32[32,2,72,4]{2,0,3,1:T(8,128)}, f32[32,2,72,4]{2,0,3,1:T(8,128)}, u32[]{:S(2)}, u32[]{:S(2)}) collective-permute-start(f32[32,2,72,4]{2,0,3,1:T(8,128)} %copy.50), channel_id=1, source_target_pairs={{0,1},{1,2},{2,3},{4,5},{5,6},{6,7},{8,9},{9,10},{10,11},{12,13},{... | collective-permute-start | bytes 221192 | tf_op jit(solution)/shard_map/ppermute | solution.py:21
  214.3 5.4 %collective-permute-start.11 = (f32[32,2,72,4]{2,0,3,1:T(8,128)}, f32[32,2,72,4]{2,0,3,1:T(8,128)}, u32[]{:S(2)}, u32[]{:S(2)}) collective-permute-start(f32[32,2,72,4]{2,0,3,1:T(8,128)} %copy.51), channel_id=1, source_target_pairs={{1,0},{2,1},{3,2},{5,4},{6,5},{7,6},{9,8},{10,9},{11,10},{13,12},{... | collective-permute-start | bytes 221192 | tf_op jit(solution)/shard_map/ppermute | solution.py:23
  335.9 11.1 %copy-start = (f32[32,2,64,128]{3,0,2,1:T(8,128)}, f32[32,2,64,128]{3,0,2,1:T(8,128)S(1)}, u32[]{:S(2)}) copy-start(f32[32,2,64,128]{3,0,2,1:T(8,128)S(1)} %broadcast_divide_fusion) | copy-start | bytes 6291460
  335.9 6.7 %collective-permute-start.12 = (f32[32,2,4,128]{3,0,2,1:T(8,128)S(1)}, f32[32,2,4,128]{3,0,2,1:T(8,128)S(1)}, u32[]{:S(2)}, u32[]{:S(2)}) collective-permute-start(f32[32,2,4,128]{3,0,2,1:T(8,128)S(1)} %get-tuple-element.26), channel_id=1, source_target_pairs={{0,4},{4,8},{8,12},{12,16},{16,20},{20,24},{24,28},{1,5},{5,9},{9,... | collective-permute-start | bytes 393224 | tf_op jit(solution)/shard_map/ppermute | solution.py:21
  340.1 6.9 %collective-permute-start.13 = (f32[32,2,4,128]{3,0,2,1:T(8,128)S(1)}, f32[32,2,4,128]{3,0,2,1:T(8,128)S(1)}, u32[]{:S(2)}, u32[]{:S(2)}) collective-permute-start(f32[32,2,4,128]{3,0,2,1:T(8,128)S(1)} %get-tuple-element.27), channel_id=1, source_target_pairs={{4,0},{8,4},{12,8},{16,12},{20,16},{24,20},{28,24},{5,1},{9,5},{13... | collective-permute-start | bytes 393224 | tf_op jit(solution)/shard_map/ppermute | solution.py:23
  342.6 4.4 copy-start.7
  347.0 0.6 copy-start.9
  354.3 6.7 %collective-permute-start.14 = (f32[32,2,72,4]{2,0,3,1:T(8,128)}, f32[32,2,72,4]{2,0,3,1:T(8,128)}, u32[]{:S(2)}, u32[]{:S(2)}) collective-permute-start(f32[32,2,72,4]{2,0,3,1:T(8,128)} %copy.54), channel_id=1, source_target_pairs={{0,1},{1,2},{2,3},{4,5},{5,6},{6,7},{8,9},{9,10},{10,11},{12,13},{... | collective-permute-start | bytes 221192 | tf_op jit(solution)/shard_map/ppermute | solution.py:21
  359.7 5.4 %collective-permute-start.15 = (f32[32,2,72,4]{2,0,3,1:T(8,128)}, f32[32,2,72,4]{2,0,3,1:T(8,128)}, u32[]{:S(2)}, u32[]{:S(2)}) collective-permute-start(f32[32,2,72,4]{2,0,3,1:T(8,128)} %copy.55), channel_id=1, source_target_pairs={{1,0},{2,1},{3,2},{5,4},{6,5},{7,6},{9,8},{10,9},{11,10},{13,12},{... | collective-permute-start | bytes 221192 | tf_op jit(solution)/shard_map/ppermute | solution.py:23
  426.0 10.9 %copy-start.3 = (f32[32,2,64,128]{3,0,2,1:T(8,128)}, f32[32,2,64,128]{3,0,2,1:T(8,128)S(1)}, u32[]{:S(2)}) copy-start(f32[32,2,64,128]{3,0,2,1:T(8,128)S(1)} %convert_multiply_fusion) | copy-start | bytes 6291460
  426.0 6.5 %collective-permute-start.16 = (f32[32,2,4,128]{3,0,2,1:T(8,128)S(1)}, f32[32,2,4,128]{3,0,2,1:T(8,128)S(1)}, u32[]{:S(2)}, u32[]{:S(2)}) collective-permute-start(f32[32,2,4,128]{3,0,2,1:T(8,128)S(1)} %get-tuple-element.24), channel_id=1, source_target_pairs={{0,4},{4,8},{8,12},{12,16},{16,20},{20,24},{24,28},{1,5},{5,9},{9,... | collective-permute-start | bytes 393224 | tf_op jit(solution)/shard_map/ppermute | solution.py:21
  430.0 6.9 %collective-permute-start.17 = (f32[32,2,4,128]{3,0,2,1:T(8,128)S(1)}, f32[32,2,4,128]{3,0,2,1:T(8,128)S(1)}, u32[]{:S(2)}, u32[]{:S(2)}) collective-permute-start(f32[32,2,4,128]{3,0,2,1:T(8,128)S(1)} %get-tuple-element.25), channel_id=1, source_target_pairs={{4,0},{8,4},{12,8},{16,12},{20,16},{24,20},{28,24},{5,1},{9,5},{13... | collective-permute-start | bytes 393224 | tf_op jit(solution)/shard_map/ppermute | solution.py:23
  442.9 8.2 %collective-permute-start.18 = (f32[32,2,72,4]{2,0,3,1:T(8,128)S(1)}, f32[32,2,72,4]{2,0,3,1:T(8,128)S(1)}, u32[]{:S(2)}, u32[]{:S(2)}) collective-permute-start(f32[32,2,72,4]{2,0,3,1:T(8,128)S(1)} %copy.60), channel_id=1, source_target_pairs={{0,1},{1,2},{2,3},{4,5},{5,6},{6,7},{8,9},{9,10},{10,11},{12,13},{... | collective-permute-start | bytes 221192 | tf_op jit(solution)/shard_map/ppermute | solution.py:21
  449.8 5.3 collective-permute-start.19
  473.0 4.7 copy-start.1
where the time goes:
time: 542 us; the launch traced here: 534 us
  blocking collectives  169 us (31%)
  other arithmetic  165 us (30%)
  local copies, waits for them, and re-layouts  121 us (22%)
  starting transfers between devices  47.1 us (9%)
  waiting for transfers between devices  28 us (5%)
    mul x19, other arithmetic, filtered(): padded = padded * (row_keep[:, None] * col_keep[None, :])  72.4 us
    psum x1, blocking collectives, on_device(): bnorm = jnp.sqrt(lax.psum(jnp.sum(gradient * gradient), ('gy', 'gx')) + EPS)  44.1 us
    psum x1, blocking collectives, on_device(): alpha_two = lax.psum(jnp.sum(second * image_two), ('gy', 'gx'))  42.8 us
    psum x1, blocking collectives, on_device(): alpha_one = lax.psum(jnp.sum(first * image_one), ('gy', 'gx'))  42.5 us
    psum x1, blocking collectives, on_device(): beta_sq = lax.psum(jnp.sum(remain * remain), ('gy', 'gx'))  39.4 us
    scatter-add x3, other arithmetic, adjoint_obs(): jnp.zeros((levels * rows * cols,), jnp.float32).at[points].add(values)  35.3 us
    ppermute x10, starting transfers between devices, with_halo(): lax.ppermute(tail, axis, [(i, (i + 1) % count) for i in range(ends)])  34.1 us
    gather x2, local copies, waits for them, and re-layouts, hessian(): seen = state.reshape(-1)[points]  32.3 us
  transfers between devices with their start and end apart: 20, of which 12 were waited for; matrix products, arithmetic and copies ran while one was open for 6% of the time, Pallas kernels for 0%

commit v1 on v0

v1 whole, which is shorter than its diff:
```python
import functools
import jax
import jax.numpy as jnp
from jax import lax
from jax.experimental import pallas as pl
from jax.experimental.pallas import tpu as pltpu
from jax.sharding import PartitionSpec as P

SWEEPS = 4
KAPPA = 0.2
EPS = 1e-06
W = 2 * SWEEPS
KEEP = 3 * W
HALF = 64


def scatter_kernel(cell_ref, level_ref, inn_ref, wt_ref, g_ref, d_ref, *, rows, cols):
    cell = cell_ref[...]
    row = level_ref[...] * rows + cell // cols
    col = cell % cols
    n = cell.shape[1]
    lr = g_ref.shape[0]
    hot = jnp.where(lax.broadcasted_iota(jnp.int32, (lr, n), 0) == row, 1.0, 0.0).astype(jnp.bfloat16)
    at = lax.broadcasted_iota(jnp.int32, (cols, n), 0) == col
    wt = wt_ref[...]
    for ref, v in ((g_ref, wt * inn_ref[...]), (d_ref, wt)):
        hi = v.astype(jnp.bfloat16).astype(jnp.float32)
        lo = v - hi
        total = None
        for part in (hi, lo):
            sel = jnp.where(at, part, 0.0).astype(jnp.bfloat16)
            term = lax.dot_general(hot, sel, (((1,), (1,)), ((), ())), preferred_element_type=jnp.float32)
            total = term if total is None else total + term
        ref[...] = total


def fill_kappa(km_ref, ks_ref, rows, cols):
    hr = km_ref.shape[0]
    gy, gx = lax.axis_index("gy"), lax.axis_index("gx")
    r = lax.broadcasted_iota(jnp.int32, (hr, cols), 0) + gy * rows - W
    rok = (r >= 0) & (r < rows * lax.axis_size("gy"))
    km_ref[...] = jnp.where(rok, KAPPA, 0.0)
    lane = lax.broadcasted_iota(jnp.int32, (hr, cols), 1) % HALF
    west = lane < KEEP
    c = jnp.where(west, lane - W, lane - HALF // 2 + cols - 2 * W) + gx * cols
    real = west | ((lane >= HALF // 2) & (lane < HALF // 2 + KEEP))
    cok = real & (c >= 0) & (c < cols * lax.axis_size("gx"))
    ks_ref[...] = jnp.where(rok & cok, KAPPA, 0.0)


def g_kernel(e_ref, s_ref, g_ref, gs_ref, p_ref, ps_ref, y_ref, km_ref, ks_ref, ym_ref, yst_ref,
             *, members, levels, rows, cols):
    hr = rows + 2 * W
    groups = members // 8
    pairs = groups // 2
    fill_kappa(km_ref, ks_ref, rows, cols)

    def e_row(l, m, r):
        return e_ref[pl.ds(((m * 8) * levels + l) * hr + r, 8, stride=levels * hr), :]

    def s_row(l, j, r):
        return s_ref[pl.ds(((l * pairs + j) * 8) * hr + r, 8, stride=hr), :]

    def sweep_all(state, vals, r):
        new = []
        for s in range(SWEEPS):
            km = km_ref[pl.ds(jnp.maximum(r - s - 1, 0), 1), :]
            ks = ks_ref[pl.ds(jnp.maximum(r - s - 1, 0), 1), :]
            out = []
            for c, u in enumerate(vals):
                q, prev = state[s][c]
                out.append((km if c < groups else ks) * (q + u))
                h = u + prev + (pltpu.roll(u, 1, 1) + pltpu.roll(u, cols - 1, 1))
                new.append((h, u))
            vals = out
        n = len(vals)
        return [new[s * n:(s + 1) * n] for s in range(SWEEPS)], vals

    count = groups + pairs
    zero = jnp.zeros((8, cols), jnp.float32)
    for l in range(levels):
        start = [[(zero, zero)] * count for _ in range(SWEEPS)]

        def first(r, state):
            gm = g_ref[l, pl.ds(r, 1), :]
            gs = gs_ref[l, pl.ds(r, 1), :]
            vals = [e_row(l, m, r) * gm for m in range(groups)] + [s_row(l, j, r) * gs for j in range(pairs)]
            state, vals = sweep_all(state, vals, r)
            o = jnp.maximum(r - SWEEPS, 0)
            for m in range(groups):
                p_ref[l * groups + m, o] = vals[m]
            for j in range(pairs):
                ps_ref[l * pairs + j, o] = vals[groups + j]
            return state

        lax.fori_loop(0, hr, first, start)

        def second(r, state):
            vals = [p_ref[l * groups + m, r] for m in range(groups)] + [ps_ref[l * pairs + j, r] for j in range(pairs)]
            state, vals = sweep_all(state, vals, r)
            o = jnp.maximum(r - SWEEPS, 0)
            acc = None
            for m in range(groups):
                t = vals[m] * e_row(l, m, o)
                acc = t if acc is None else acc + t
            ym_ref[l, o] = acc
            acc = None
            for j in range(pairs):
                t = vals[groups + j] * s_row(l, j, o)
                acc = t if acc is None else acc + t
            yst_ref[l, o] = acc
            return state

        lax.fori_loop(SWEEPS, hr - SWEEPS, second, start)
    lane = lax.broadcasted_iota(jnp.int32, (rows, cols), 1)
    for l in range(levels):
        main = jnp.sum(ym_ref[l, W:W + rows], axis=1)
        st = jnp.sum(yst_ref[l, W:W + rows], axis=1)
        st = st + pltpu.roll(st, HALF, 1)
        west = pltpu.roll(st, cols - W, 1)
        east = pltpu.roll(st, cols - W - (HALF // 2 + W), 1)
        y_ref[l] = jnp.where(lane < W, west, jnp.where(lane >= cols - W, east, main))


def g_apply(e2, s2, gm, gs, dims):
    members, levels, rows, cols = dims
    hr = rows + 2 * W
    groups = members // 8
    pairs = groups // 2
    vm = pl.BlockSpec(memory_space=pltpu.VMEM)
    f32 = jnp.float32
    return pl.pallas_call(
        functools.partial(g_kernel, members=members, levels=levels, rows=rows, cols=cols),
        out_shape=(
            jax.ShapeDtypeStruct((levels * groups, hr, 8, cols), f32),
            jax.ShapeDtypeStruct((levels * pairs, hr, 8, cols), f32),
            jax.ShapeDtypeStruct((levels, rows, cols), f32),
        ),
        in_specs=[vm] * 4,
        out_specs=(vm,) * 3,
        scratch_shapes=[pltpu.VMEM((hr, cols), f32), pltpu.VMEM((hr, cols), f32),
                        pltpu.VMEM((levels, hr, 8, cols), f32), pltpu.VMEM((levels, hr, 8, cols), f32)],
        compiler_params=pltpu.CompilerParams(vmem_limit_bytes=60000000),
    )(e2, s2, gm, gs)


def with_halo(cells, sides, width):
    for axis, dim in sides:
        count = lax.axis_size(axis)
        ends = count - 1
        head = lax.slice_in_dim(cells, 0, width, axis=dim)
        tail = lax.slice_in_dim(cells, cells.shape[dim] - width, cells.shape[dim], axis=dim)
        cells = jnp.concatenate(
            [
                lax.ppermute(tail, axis, [(i, (i + 1) % count) for i in range(ends)]),
                cells,
                lax.ppermute(head, axis, [((i + 1) % count, i) for i in range(ends)]),
            ],
            axis=dim,
        )
    return cells


def strip_of(full, cols):
    pad = jnp.zeros(full.shape[:-1] + (HALF // 2 - KEEP,), full.dtype)
    return jnp.concatenate([full[..., :KEEP], pad, full[..., full.shape[-1] - KEEP:], pad], axis=-1)


def on_device(ensemble, obs_cell, obs_level, innovation, obs_weight):
    members, levels, rows, cols = ensemble.shape
    groups = members // 8
    pairs = groups // 2
    hr = rows + 2 * W
    f32 = jnp.float32
    vm = pl.BlockSpec(memory_space=pltpu.VMEM)
    flat = lambda a: a.reshape(1, -1)
    g0, dd = pl.pallas_call(
        functools.partial(scatter_kernel, rows=rows, cols=cols),
        out_shape=(jax.ShapeDtypeStruct((levels * rows, cols), f32),) * 2,
        in_specs=[vm] * 4, out_specs=(vm, vm),
    )(flat(obs_cell), flat(obs_level), flat(innovation), flat(obs_weight))
    g0 = g0.reshape(levels, rows, cols)
    dd = dd.reshape(levels, rows, cols)
    full = with_halo(ensemble.astype(f32), (("gy", 2), ("gx", 3)), W)
    e2 = full[..., W:W + cols].reshape(members * levels * hr, cols)
    st = strip_of(full, cols)
    st = st.reshape(pairs, 2, 8, levels, hr, HALF).transpose(3, 0, 2, 4, 1, 5)
    s2 = st.reshape(levels * pairs * 8 * hr, cols)

    def apply(g):
        gf = with_halo(g, (("gy", 1), ("gx", 2)), W)
        gs = strip_of(gf, cols)
        return g_apply(e2, s2, gf[..., W:W + cols], jnp.concatenate([gs, gs], -1), ensemble.shape)

    p0, ps0, y0 = apply(g0)
    g1 = dd * y0
    p1, ps1, y1 = apply(g1)
    sums = jnp.stack([jnp.sum(g0 * y0), jnp.sum(g1 * y0), jnp.sum(g1 * y1), jnp.sum(dd * y1 * y1)])
    m = lax.psum(sums, ("gy", "gx"))
    bn2 = m[0] + EPS
    c = (EPS - m[1]) / bn2
    alpha1 = (m[0] + m[1]) / bn2
    r2 = jnp.maximum((c * c * m[0] + 2.0 * c * m[1] + m[2]) / bn2, 0.0)
    rho = (c * c * m[1] + 2.0 * c * m[2] + m[3]) / bn2
    b2 = r2 + EPS
    alpha2 = (r2 + rho) / b2
    det = alpha1 * alpha2 - b2
    ca = (alpha2 - c) / det
    cb = -1.0 / det

    pm = ca * p0[:, W:W + rows] + cb * p1[:, W:W + rows]
    ps = ca * ps0[:, W:W + rows] + cb * ps1[:, W:W + rows]
    pm = pm.reshape(levels, pairs, 2, rows, 8, cols).transpose(1, 2, 4, 0, 3, 5).reshape(members, levels, rows, cols)
    ps = ps.reshape(levels, pairs, rows, 8, 2, HALF).transpose(1, 4, 3, 0, 2, 5).reshape(members, levels, rows, HALF)
    control = jnp.concatenate([ps[..., W:2 * W], pm[..., W:cols - W], ps[..., HALF // 2 + W:HALF // 2 + 2 * W]], -1)
    increment = ca * y0 + cb * y1
    return (control, increment)


def solution(mesh):
    return jax.shard_map(
        on_device,
        mesh=mesh,
        in_specs=(
            P(None, None, "gy", "gx"),
            P("gy", "gx", None),
            P("gy", "gx", None),
            P("gy", "gx", None),
            P("gy", "gx", None),
        ),
        out_specs=(P(None, None, "gy", "gx"), P(None, "gy", "gx")),
        check_vma=False,
    )
```

time: 542 us -> 234 us (0.43); the launches traced: 534 us -> 232 us
  other arithmetic: 165 us -> 19.9 us
  blocking collectives: 169 us -> 47.1 us
  local copies, waits for them, and re-layouts: 121 us -> 31.8 us
  Pallas kernels: 0 us -> 87.8 us
  waiting for transfers between devices: 28 us -> 3.14 us
  starting transfers between devices: 47.1 us -> 35 us
    psum x4 -> x1, blocking collectives: 169 us -> 47.1 us  [on_device(): m = lax.psum(sums, ('gy', 'gx'))]
    pallas_call x0 -> x3, Pallas kernels: none -> 87.8 us  [the longest x2 85.7 us: g_apply(): pl.pallas_call(functools.partial(g_kernel, members=members, levels=levels...]
    mul x25 -> x1, other arithmetic: 78.7 us -> 0.85 us  [on_device(): g1 = dd * y0]
    scatter-add x3 -> x0, other arithmetic: 35.3 us -> none  [adjoint_obs(): jnp.zeros((levels * rows * cols,), jnp.float32).at[points].add(values)]
    gather x2 -> x0, local copies, waits for them, and re-layouts: 32.3 us -> none  [hessian(): seen = state.reshape(-1)[points]]
    concatenate x10 -> x5, other arithmetic: 25.9 us -> 1.24 us  [with_halo(): jnp.concatenate([lax.ppermute(tail, axis, [(i, (i + 1) % count) for i in...]
    slice x15 -> x5, local copies, waits for them, and re-layouts: 30.5 us -> 6.45 us  [with_halo(): lax.slice_in_dim(cells, cells.shape[dim] - width, cells.shape[dim], axis=...]
    ppermute x10 -> x6, waiting for transfers between devices: 21.4 us -> 0.02 us  [with_halo(): lax.ppermute(head, axis, [((i + 1) % count, i) for i in range(ends)])]
  transfers between devices with their start and end apart: 20 -> 12, of which waited for: 12 -> 3; matrix products, arithmetic and copies ran while one was open for 6% -> 4% of each run, Pallas kernels for 0% -> 1%
where the time goes in v1:
time: 234 us; the launch traced here: 232 us
  Pallas kernels  87.8 us (38%)
  blocking collectives  47.1 us (20%)
  starting transfers between devices  35 us (15%)
  local copies, waits for them, and re-layouts  31.8 us (14%)
  other arithmetic  19.9 us (9%)
  between operations  7.74 us (3%)
  waiting for transfers between devices  3.14 us (1%)
    pallas_call x2, Pallas kernels, g_apply(): pl.pallas_call(functools.partial(g_kernel, members=members, levels=levels...  85.7 us
    psum x1, blocking collectives, on_device(): m = lax.psum(sums, ('gy', 'gx'))  47.1 us
    ppermute x6, starting transfers between devices, with_halo(): lax.ppermute(tail, axis, [(i, (i + 1) % count) for i in range(ends)])  27.2 us
    ppermute x6, starting transfers between devices, with_halo(): lax.ppermute(head, axis, [((i + 1) % count, i) for i in range(ends)])  7.76 us
    concatenate x1, other arithmetic, strip_of(): jnp.concatenate([full[..., :KEEP], pad, full[..., full.shape[-1] - KEEP:]...  6.59 us
    slice x5, local copies, waits for them, and re-layouts, with_halo(): lax.slice_in_dim(cells, cells.shape[dim] - width, cells.shape[dim], axis=...  6.45 us
  transfers between devices with their start and end apart: 12, of which 3 were waited for; matrix products, arithmetic and copies ran while one was open for 4% of the time, Pallas kernels for 1%

profile of v1, /device:TPU:0, one launch (start us, length us, event | category | flops | bytes accessed | tf_op | source)
XLA Modules:
  0.0 232.4 jit_solution(17249039457762694943)
XLA Ops:
  0.6 1.0 fusion.7
  1.6 1.3 collective-permute-start.1
  2.9 5.5 %collective-permute-start = (f32[32,2,8,128]{3,2,1,0:T(8,128)S(1)}, f32[32,2,8,128]{3,2,1,0:T(8,128)S(1)}, u32[]{:S(2)}, u32[]{:S(2)}) collective-permute-start(f32[32,2,8,128]{3,2,1,0:T(8,128)S(1)} %get-tuple-element.26), channel_id=1, source_target_pairs={{0,4},{4,8},{8,12},{12,16},{16,20},{20,24},{24,28},{1,5},{5,9},{9,... | collective-permute-start | bytes 786440 | tf_op jit(solution)/shard_map/ppermute | solution.py:155
  8.5 2.1 shard_map.68
  10.6 0.8 fusion.11
  11.4 1.3 collective-permute-start.5
  12.7 5.4 %collective-permute-start.4 = (f32[2,8,128]{2,1,0:T(8,128)S(1)}, f32[2,8,128]{2,1,0:T(8,128)S(1)}, u32[]{:S(2)}, u32[]{:S(2)}) collective-permute-start(f32[2,8,128]{2,1,0:T(8,128)S(1)} %get-tuple-element.38), channel_id=1, source_target_pairs={{0,4},{4,8},{8,12},{12,16},{16,20},{20,24},{24,28},{1,5},{5,9},{9,... | collective-permute-start | bytes 24584 | tf_op jit(solution)/shard_map/ppermute | solution.py:155
  18.1 1.5 convert_element_type.3
  19.7 1.2 copy-done.1
  21.1 3.2 %fusion.5 = (f32[32,2,80,8]{3,2,1,0:T(8,128)}, f32[32,2,80,8]{3,2,1,0:T(8,128)}) fusion(f32[32,2,80,128]{3,2,1,0:T(8,128)S(1)} %pad_maximum_fusion.2), kind=kLoop, calls=%fused_computation.39 | loop fusion | bytes 655360 | tf_op jit(solution)/shard_map/slice | solution.py:152
  24.4 2.6 %copy.24 = f32[32,2,80,8]{2,3,1,0:T(8,128)S(1)} copy(f32[32,2,80,8]{3,2,1,0:T(8,128)} %get-tuple-element.23) | data formatting | bytes 327680 | tf_op jit(solution)/shard_map/slice | solution.py:151
  26.9 1.3 collective-permute-start.3
  28.3 1.4 copy.22
  29.7 3.0 %collective-permute-start.2 = (f32[32,2,80,8]{2,3,1,0:T(8,128)}, f32[32,2,80,8]{2,3,1,0:T(8,128)S(1)}, u32[]{:S(2)}, u32[]{:S(2)}) collective-permute-start(f32[32,2,80,8]{2,3,1,0:T(8,128)} %copy.22), channel_id=1, source_target_pairs={{0,1},{1,2},{2,3},{4,5},{5,6},{6,7},{8,9},{9,10},{10,11},{12,13},{... | collective-permute-start | bytes 491528 | tf_op jit(solution)/shard_map/ppermute | solution.py:155
  32.8 1.3 collective-permute-start.7
  34.1 3.7 %collective-permute-start.6 = (f32[2,80,8]{2,1,0:T(8,128)S(1)}, f32[2,80,8]{2,1,0:T(8,128)S(1)}, u32[]{:S(2)}, u32[]{:S(2)}) collective-permute-start(f32[2,80,8]{2,1,0:T(8,128)S(1)} %get-tuple-element.35), channel_id=1, source_target_pairs={{0,1},{1,2},{2,3},{4,5},{5,6},{6,7},{8,9},{9,10},{10,11},{12,13},{... | collective-permute-start | bytes 15368 | tf_op jit(solution)/shard_map/ppermute | solution.py:155
  37.8 0.9 collective-permute-done.6
  38.7 0.9 pad_maximum_fusion.10
  39.6 0.9 concatenate.53.gs_ref
  40.5 3.3 %copy.25 = f32[32,2,80,8]{3,2,1,0:T(8,128)} copy(f32[32,2,80,8]{2,3,1,0:T(8,128)} %collective-permute-done.3) | data formatting | bytes 327680 | tf_op jit(solution)/shard_map/ppermute | solution.py:157
  43.8 2.2 copy.23
  46.3 1.4 copy-done.4
  47.8 6.6 %fusion.1 = f32[32,2,80,64]{3,2,1,0:T(8,128)} fusion(f32[32,2,80,8]{3,2,1,0:T(8,128)S(1)} %copy-done.4, f32[32,2,8,128]{3,2,1,0:T(8,128)S(1)} %collective-permute-done.1, f32[32,2,64,128]{3,2,1,0:T(8,128)S(1)} %copy-done.2, f32[32,2,8,128]{3,2,1,0:T(8,128)S(1)} %collective-permute-done, f32[32,2,80,8]{3,2,1,0:T(8,128)} %copy.23, ...), kind=kLoop, calls=%fused_computation.4 | loop fusion | flops 6225920 | bytes 4423680 | tf_op jit(solution)/shard_map/concatenate | solution.py:166
  54.4 3.3 %copy.26 = f32[2,2,8,2,80,64]{4,2,0,3,5,1:T(8,128)S(1)} copy(f32[2,2,8,2,80,64]{5,4,3,2,1,0:T(8,128)} %bitcast.33) | data formatting | bytes 2621440 | tf_op jit(solution)/shard_map/reshape | solution.py:187
  57.6 1.7 reshape.50
  59.4 1.5 copy.27.s_ref
  60.8 42.9 %shard_map.69 = (f32[8,80,8,128]{3,2,1,0:T(8,128)}, f32[4,80,8,128]{3,2,1,0:T(8,128)}, f32[2,64,128]{2,1,0:T(8,128)}) custom-call(f32[5120,128]{1,0:T(8,128)} %bitcast.30, f32[2560,128]{1,0:T(8,128)} %copy.27.s_ref, f32[2,80,128]{2,1,0:T(8,128)} %copy-done.7, f32[2,80,128]{2,1,0:T(8,128)} %concatenate.53.gs_ref), custom_call_target="tpu_custom_call" | custom-call | tf_op jit(solution)/shard_map/pallas_call | solution.py:132
  103.8 0.8 bitcast_multiply_fusion
  104.6 1.3 collective-permute-start.9
  105.9 5.4 %collective-permute-start.8 = (f32[2,8,128]{2,1,0:T(8,128)S(1)}, f32[2,8,128]{2,1,0:T(8,128)S(1)}, u32[]{:S(2)}, u32[]{:S(2)}) collective-permute-start(f32[2,8,128]{2,1,0:T(8,128)S(1)} %get-tuple-element.36), channel_id=1, source_target_pairs={{0,4},{4,8},{8,12},{12,16},{16,20},{20,24},{24,28},{1,5},{5,9},{9,... | collective-permute-start | bytes 24584 | tf_op jit(solution)/shard_map/ppermute | solution.py:155
  111.4 1.3 collective-permute-done.8
  112.8 1.3 collective-permute-start.11
  114.1 4.1 %collective-permute-start.10 = (f32[2,80,8]{2,1,0:T(8,128)S(1)}, f32[2,80,8]{2,1,0:T(8,128)S(1)}, u32[]{:S(2)}, u32[]{:S(2)}) collective-permute-start(f32[2,80,8]{2,1,0:T(8,128)S(1)} %get-tuple-element.31), channel_id=1, source_target_pairs={{0,1},{1,2},{2,3},{4,5},{5,6},{6,7},{8,9},{9,10},{10,11},{12,13},{... | collective-permute-start | bytes 15368 | tf_op jit(solution)/shard_map/ppermute | solution.py:155
  118.3 0.9 collective-permute-done.10
  119.3 0.8 concatenate.57.gs_ref
  120.1 42.7 %shard_map.70 = (f32[8,80,8,128]{3,2,1,0:T(8,128)}, f32[4,80,8,128]{3,2,1,0:T(8,128)}, f32[2,64,128]{2,1,0:T(8,128)}) custom-call(f32[5120,128]{1,0:T(8,128)} %bitcast.31, f32[2560,128]{1,0:T(8,128)} %copy.27.s_ref, f32[2,80,128]{2,1,0:T(8,128)} %copy-done.8, f32[2,80,128]{2,1,0:T(8,128)} %concatenate.57.gs_ref), custom_call_target="tpu_custom_call" | custom-call | tf_op jit(solution)/shard_map/pallas_call | solution.py:132
  162.9 1.5 multiply_reduce_fusion.2
  164.4 2.7 %pad_maximum_fusion.18 = f32[4]{0:T(128)S(1)} fusion(f32[1]{0:T(128)} %bitcast.12, f32[1]{0:T(128)} %bitcast.11, f32[1]{0:T(128)} %bitcast.10, f32[1]{0:T(128)} %bitcast.8), kind=kLoop, calls=%fused_computation.37 | loop fusion | flops 12 | bytes 32 | tf_op jit(solution)/shard_map/stack | solution.py:198
  167.1 47.1 %psum.7 = f32[4]{0:T(128)S(1)} all-reduce(f32[4]{0:T(128)S(1)} %pad_maximum_fusion.18), channel_id=1, replica_groups=mesh['gy'=8,'gx'=4] {'gy','gx'}, use_global_device_ids=true, to_apply=%region_4.0 | all-reduce | flops 4 | bytes 32 | tf_op jit(solution)/shard_map/psum | solution.py:199
  214.2 0.7 fusion.12
  221.6 1.5 multiply_add_fusion.2
  223.1 1.3 multiply_add_fusion.1
  224.4 1.2 reshape.52
  225.6 0.6 copy.29
  226.2 1.1 fusion.6
  228.0 0.8 copy-done.6
  229.4 0.6 slice.141
  230.0 2.5 %pad_maximum_fusion.3 = f32[32,2,64,128]{3,2,1,0:T(8,128)} fusion(f32[32,2,64,8]{3,2,1,0:T(8,128)S(1)} %get-tuple-element.25, f32[32,2,64,112]{3,2,1,0:T(8,128)S(1)} %slice.141, f32[32,2,64,8]{3,2,1,0:T(8,128)S(1)} %get-tuple-element.24), kind=kLoop, calls=%fused_computation.14 | loop fusion | flops 1048576 | bytes 4194304 | tf_op jit(solution)/shard_map/concatenate | solution.py:215
  (47 shorter events, 2.1 us)
Async XLA Ops:
  1.6 18.0 %collective-permute-start.1 = (f32[32,2,8,128]{3,2,1,0:T(8,128)S(1)}, f32[32,2,8,128]{3,2,1,0:T(8,128)S(1)}, u32[]{:S(2)}, u32[]{:S(2)}) collective-permute-start(f32[32,2,8,128]{3,2,1,0:T(8,128)S(1)} %get-tuple-element.27), channel_id=1, source_target_pairs={{4,0},{8,4},{12,8},{16,12},{20,16},{24,20},{28,24},{5,1},{9,5},{13... | collective-permute-start | bytes 786440 | tf_op jit(solution)/shard_map/ppermute | solution.py:157
  2.9 16.7 %collective-permute-start = (f32[32,2,8,128]{3,2,1,0:T(8,128)S(1)}, f32[32,2,8,128]{3,2,1,0:T(8,128)S(1)}, u32[]{:S(2)}, u32[]{:S(2)}) collective-permute-start(f32[32,2,8,128]{3,2,1,0:T(8,128)S(1)} %get-tuple-element.26), channel_id=1, source_target_pairs={{0,4},{4,8},{8,12},{12,16},{16,20},{20,24},{24,28},{1,5},{5,9},{9,... | collective-permute-start | bytes 786440 | tf_op jit(solution)/shard_map/ppermute | solution.py:155
  10.6 9.0 %copy-start.10 = (f32[128,128]{1,0:T(8,128)S(1)}, f32[128,128]{1,0:T(8,128)}, u32[]{:S(2)}) copy-start(f32[128,128]{1,0:T(8,128)} %get-tuple-element.10) | copy-start | bytes 196612
  11.4 8.2 %collective-permute-start.5 = (f32[2,8,128]{2,1,0:T(8,128)S(1)}, f32[2,8,128]{2,1,0:T(8,128)S(1)}, u32[]{:S(2)}, u32[]{:S(2)}) collective-permute-start(f32[2,8,128]{2,1,0:T(8,128)S(1)} %get-tuple-element.39), channel_id=1, source_target_pairs={{4,0},{8,4},{12,8},{16,12},{20,16},{24,20},{28,24},{5,1},{9,5},{13... | collective-permute-start | bytes 24584 | tf_op jit(solution)/shard_map/ppermute | solution.py:157
  12.7 6.9 %collective-permute-start.4 = (f32[2,8,128]{2,1,0:T(8,128)S(1)}, f32[2,8,128]{2,1,0:T(8,128)S(1)}, u32[]{:S(2)}, u32[]{:S(2)}) collective-permute-start(f32[2,8,128]{2,1,0:T(8,128)S(1)} %get-tuple-element.38), channel_id=1, source_target_pairs={{0,4},{4,8},{8,12},{12,16},{16,20},{20,24},{24,28},{1,5},{5,9},{9,... | collective-permute-start | bytes 24584 | tf_op jit(solution)/shard_map/ppermute | solution.py:155
  19.6 1.3 copy-start.1
  19.6 1.5 copy-start.13
  19.6 1.5 copy-start.14
  19.6 13.1 %copy-start.7 = (f32[2,80,128]{2,1,0:T(8,128)}, f32[2,80,128]{2,1,0:T(8,128)S(1)}, u32[]{:S(2)}) copy-start(f32[2,80,128]{2,1,0:T(8,128)S(1)} %pad_maximum_fusion.16.g_ref) | copy-start | bytes 245764
  21.1 3.2 %copy-start = (f32[32,2,80,128]{3,2,1,0:T(8,128)}, f32[32,2,80,128]{3,2,1,0:T(8,128)S(1)}, u32[]{:S(2)}) copy-start(f32[32,2,80,128]{3,2,1,0:T(8,128)S(1)} %pad_maximum_fusion.2) | copy-start | bytes 7864324
  24.4 3.9 %copy-start.3 = (f32[32,2,80,8]{3,2,1,0:T(8,128)S(1)}, f32[32,2,80,8]{3,2,1,0:T(8,128)}, u32[]{:S(2)}) copy-start(f32[32,2,80,8]{3,2,1,0:T(8,128)} %get-tuple-element.22) | copy-start | bytes 491524
  26.9 13.6 %collective-permute-start.3 = (f32[32,2,80,8]{2,3,1,0:T(8,128)S(1)}, f32[32,2,80,8]{2,3,1,0:T(8,128)}, u32[]{:S(2)}, u32[]{:S(2)}) collective-permute-start(f32[32,2,80,8]{2,3,1,0:T(8,128)S(1)} %copy.24), channel_id=1, source_target_pairs={{1,0},{2,1},{3,2},{5,4},{6,5},{7,6},{9,8},{10,9},{11,10},{13,12},{... | collective-permute-start | bytes 491528 | tf_op jit(solution)/shard_map/ppermute | solution.py:157
  29.7 14.1 %collective-permute-start.2 = (f32[32,2,80,8]{2,3,1,0:T(8,128)}, f32[32,2,80,8]{2,3,1,0:T(8,128)S(1)}, u32[]{:S(2)}, u32[]{:S(2)}) collective-permute-start(f32[32,2,80,8]{2,3,1,0:T(8,128)} %copy.22), channel_id=1, source_target_pairs={{0,1},{1,2},{2,3},{4,5},{5,6},{6,7},{8,9},{9,10},{10,11},{12,13},{... | collective-permute-start | bytes 491528 | tf_op jit(solution)/shard_map/ppermute | solution.py:155
  32.8 5.0 %collective-permute-start.7 = (f32[2,80,8]{2,1,0:T(8,128)S(1)}, f32[2,80,8]{2,1,0:T(8,128)S(1)}, u32[]{:S(2)}, u32[]{:S(2)}) collective-permute-start(f32[2,80,8]{2,1,0:T(8,128)S(1)} %get-tuple-element.34), channel_id=1, source_target_pairs={{1,0},{2,1},{3,2},{5,4},{6,5},{7,6},{9,8},{10,9},{11,10},{13,12},{... | collective-permute-start | bytes 15368 | tf_op jit(solution)/shard_map/ppermute | solution.py:157
  34.1 4.6 %collective-permute-start.6 = (f32[2,80,8]{2,1,0:T(8,128)S(1)}, f32[2,80,8]{2,1,0:T(8,128)S(1)}, u32[]{:S(2)}, u32[]{:S(2)}) collective-permute-start(f32[2,80,8]{2,1,0:T(8,128)S(1)} %get-tuple-element.35), channel_id=1, source_target_pairs={{0,1},{1,2},{2,3},{4,5},{5,6},{6,7},{8,9},{9,10},{10,11},{12,13},{... | collective-permute-start | bytes 15368 | tf_op jit(solution)/shard_map/ppermute | solution.py:155
  43.8 2.5 %copy-start.2 = (f32[32,2,64,128]{3,2,1,0:T(8,128)S(1)}, f32[32,2,64,128]{3,2,1,0:T(8,128)}, u32[]{:S(2)}) copy-start(f32[32,2,64,128]{3,2,1,0:T(8,128)} %copy-done.1) | copy-start | bytes 6291460
  46.0 1.7 copy-start.4
  60.8 42.9 %copy-start.12 = (f32[128,128]{1,0:T(8,128)S(1)}, f32[128,128]{1,0:T(8,128)}, u32[]{:S(2)}) copy-start(f32[128,128]{1,0:T(8,128)} %get-tuple-element.12) | copy-start | bytes 196612
  104.6 6.8 %collective-permute-start.9 = (f32[2,8,128]{2,1,0:T(8,128)S(1)}, f32[2,8,128]{2,1,0:T(8,128)S(1)}, u32[]{:S(2)}, u32[]{:S(2)}) collective-permute-start(f32[2,8,128]{2,1,0:T(8,128)S(1)} %get-tuple-element.37), channel_id=1, source_target_pairs={{4,0},{8,4},{12,8},{16,12},{20,16},{24,20},{28,24},{5,1},{9,5},{13... | collective-permute-start | bytes 24584 | tf_op jit(solution)/shard_map/ppermute | solution.py:157
  105.9 6.8 %collective-permute-start.8 = (f32[2,8,128]{2,1,0:T(8,128)S(1)}, f32[2,8,128]{2,1,0:T(8,128)S(1)}, u32[]{:S(2)}, u32[]{:S(2)}) collective-permute-start(f32[2,8,128]{2,1,0:T(8,128)S(1)} %get-tuple-element.36), channel_id=1, source_target_pairs={{0,4},{4,8},{8,12},{12,16},{16,20},{20,24},{24,28},{1,5},{5,9},{9,... | collective-permute-start | bytes 24584 | tf_op jit(solution)/shard_map/ppermute | solution.py:155
  112.7 7.4 %copy-start.8 = (f32[2,80,128]{2,1,0:T(8,128)}, f32[2,80,128]{2,1,0:T(8,128)S(1)}, u32[]{:S(2)}) copy-start(f32[2,80,128]{2,1,0:T(8,128)S(1)} %pad_maximum_fusion.17.g_ref) | copy-start | bytes 245764
  112.8 5.4 %collective-permute-start.11 = (f32[2,80,8]{2,1,0:T(8,128)S(1)}, f32[2,80,8]{2,1,0:T(8,128)S(1)}, u32[]{:S(2)}, u32[]{:S(2)}) collective-permute-start(f32[2,80,8]{2,1,0:T(8,128)S(1)} %get-tuple-element.30), channel_id=1, source_target_pairs={{1,0},{2,1},{3,2},{5,4},{6,5},{7,6},{9,8},{10,9},{11,10},{13,12},{... | collective-permute-start | bytes 15368 | tf_op jit(solution)/shard_map/ppermute | solution.py:157
  114.1 48.8 %copy-start.11 = (f32[2,64,128]{2,1,0:T(8,128)S(1)}, f32[2,64,128]{2,1,0:T(8,128)}, u32[]{:S(2)}) copy-start(f32[2,64,128]{2,1,0:T(8,128)} %get-tuple-element.11) | copy-start | bytes 196612
  114.1 5.0 %collective-permute-start.10 = (f32[2,80,8]{2,1,0:T(8,128)S(1)}, f32[2,80,8]{2,1,0:T(8,128)S(1)}, u32[]{:S(2)}, u32[]{:S(2)}) collective-permute-start(f32[2,80,8]{2,1,0:T(8,128)S(1)} %get-tuple-element.31), channel_id=1, source_target_pairs={{0,1},{1,2},{2,3},{4,5},{5,6},{6,7},{8,9},{9,10},{10,11},{12,13},{... | collective-permute-start | bytes 15368 | tf_op jit(solution)/shard_map/ppermute | solution.py:155
  119.3 103.8 %copy-start.9 = (f32[4,80,8,128]{3,2,1,0:T(8,128)S(1)}, f32[4,80,8,128]{3,2,1,0:T(8,128)}, u32[]{:S(2)}) copy-start(f32[4,80,8,128]{3,2,1,0:T(8,128)} %get-tuple-element.14) | copy-start | bytes 3932164
  226.2 1.7 copy-start.5
  226.2 2.5 %copy-start.6 = (f32[8,80,8,128]{3,2,1,0:T(8,128)S(1)}, f32[8,80,8,128]{3,2,1,0:T(8,128)}, u32[]{:S(2)}) copy-start(f32[8,80,8,128]{3,2,1,0:T(8,128)} %get-tuple-element.17) | copy-start | bytes 7864324

commit v2 on v1

--- a/solution.py
+++ b/solution.py
@@ -1,4 +1,5 @@
 import functools
+import math
 import jax
 import jax.numpy as jnp
 from jax import lax
@@ -12,6 +13,7 @@
 W = 2 * SWEEPS
 KEEP = 3 * W
 HALF = 64
+UNROLL = 4
 
 
 def scatter_kernel(cell_ref, level_ref, inn_ref, wt_ref, g_ref, d_ref, *, rows, cols):
@@ -34,58 +36,103 @@
         ref[...] = total
 
 
-def fill_kappa(km_ref, ks_ref, rows, cols):
-    hr = km_ref.shape[0]
-    gy, gx = lax.axis_index("gy"), lax.axis_index("gx")
-    r = lax.broadcasted_iota(jnp.int32, (hr, cols), 0) + gy * rows - W
-    rok = (r >= 0) & (r < rows * lax.axis_size("gy"))
-    km_ref[...] = jnp.where(rok, KAPPA, 0.0)
-    lane = lax.broadcasted_iota(jnp.int32, (hr, cols), 1) % HALF
-    west = lane < KEEP
-    c = jnp.where(west, lane - W, lane - HALF // 2 + cols - 2 * W) + gx * cols
-    real = west | ((lane >= HALF // 2) & (lane < HALF // 2 + KEEP))
-    cok = real & (c >= 0) & (c < cols * lax.axis_size("gx"))
-    ks_ref[...] = jnp.where(rok & cok, KAPPA, 0.0)
-
-
-def g_kernel(e_ref, s_ref, g_ref, gs_ref, p_ref, ps_ref, y_ref, km_ref, ks_ref, ym_ref, yst_ref,
-             *, members, levels, rows, cols):
+def weight_kernel(wm_ref, ws_ref, *, cols):
+    i = lax.broadcasted_iota(jnp.int32, (cols, cols), 0)
+    j = lax.broadcasted_iota(jnp.int32, (cols, cols), 1)
+    near = jnp.abs(i - j) <= 1
+    gx = lax.axis_index("gx")
+
+    def real(lane):
+        lane = lane % HALF
+        west = lane < KEEP
+        c = jnp.where(west, lane - W, lane - HALF // 2 + cols - 2 * W) + gx * cols
+        inside = west | ((lane >= HALF // 2) & (lane < HALF // 2 + KEEP))
+        return inside & (c >= 0) & (c < cols * lax.axis_size("gx"))
+
+    for ref, ok in ((wm_ref, near), (ws_ref, near & real(i) & real(j))):
+        one = jnp.where(ok, 1.0, 0.0).astype(jnp.bfloat16)
+        power = one
+        for s in range(1, SWEEPS + 1):
+            if s > 1:
+                power = jnp.dot(power, one, preferred_element_type=jnp.float32).astype(jnp.bfloat16)
+            scaled = (power.astype(jnp.float32) * float(math.comb(SWEEPS, s))).astype(jnp.bfloat16)
+            ref[0:cols, (s - 1) * cols:s * cols] = scaled
+            ref[cols:2 * cols, (s - 1) * cols:s * cols] = scaled
+
+
+def g_kernel(e_ref, s_ref, g_ref, gs_ref, d_ref, wm_ref, ws_ref, p_ref, ps_ref, y_ref, km_ref, ym_ref, yst_ref,
+             u_ref, lhs_ref, f_ref, *, members, levels, rows, cols):
     hr = rows + 2 * W
     groups = members // 8
     pairs = groups // 2
-    fill_kappa(km_ref, ks_ref, rows, cols)
+    count = groups + pairs
+    scale = KAPPA ** SWEEPS
+    gy = lax.axis_index("gy")
+    rr = lax.broadcasted_iota(jnp.int32, (hr, cols), 0) + gy * rows - W
+    km_ref[...] = jnp.where((rr >= 0) & (rr < rows * lax.axis_size("gy")), 1.0, 0.0)
 
     def e_row(l, m, r):
         return e_ref[pl.ds(((m * 8) * levels + l) * hr + r, 8, stride=levels * hr), :]
 
     def s_row(l, j, r):
         return s_ref[pl.ds(((l * pairs + j) * 8) * hr + r, 8, stride=hr), :]
+
+    def ek_row(l, c, r):
+        return e_row(l, c, r) if c < groups else s_row(l, c - groups, r)
+
+    def split(c, r, u):
+        hi = u.astype(jnp.bfloat16)
+        lo = (u - hi.astype(jnp.float32)).astype(jnp.bfloat16)
+        return hi, lo
+
+    def products(lo_row, n):
+        for c in range(count):
+            w = wm_ref if c < groups else ws_ref
+            f_ref[c, pl.ds(lo_row * 8, n * 8), :] = jnp.dot(
+                lhs_ref[c, pl.ds(lo_row * 8, n * 8), :], w[...], preferred_element_type=jnp.float32)
 
     def sweep_all(state, vals, r):
         new = []
         for s in range(SWEEPS):
-            km = km_ref[pl.ds(jnp.maximum(r - s - 1, 0), 1), :]
-            ks = ks_ref[pl.ds(jnp.maximum(r - s - 1, 0), 1), :]
+            o = jnp.maximum(r - s - 1, 0)
+            km = km_ref[pl.ds(o, 1), :]
             out = []
+            at = pl.ds(pl.multiple_of(o * 8, 8), 8)
             for c, u in enumerate(vals):
-                q, prev = state[s][c]
-                out.append((km if c < groups else ks) * (q + u))
-                h = u + prev + (pltpu.roll(u, 1, 1) + pltpu.roll(u, cols - 1, 1))
-                new.append((h, u))
+                older, prev = state[s][c]
+                out.append(km * (older + u) + f_ref[c, at, s * cols:(s + 1) * cols])
+                new.append((prev, u))
             vals = out
-        n = len(vals)
-        return [new[s * n:(s + 1) * n] for s in range(SWEEPS)], vals
-
-    count = groups + pairs
-    zero = jnp.zeros((8, cols), jnp.float32)
+        return [new[s * count:(s + 1) * count] for s in range(SWEEPS)], [v * scale for v in vals]
+
+    zero = km_ref[0:8, :] * 0.0
+    start = [[(zero, zero)] * count for _ in range(SWEEPS)]
+    step = 16
+
+    def store_lhs(c, r, us):
+        his, los = zip(*[split(c, r, u) for u in us])
+        at = pl.ds(pl.multiple_of(r * 8, 16), 16)
+        lhs_ref[c, at, 0:cols] = jnp.concatenate(his, axis=0)
+        lhs_ref[c, at, cols:2 * cols] = jnp.concatenate(los, axis=0)
+
     for l in range(levels):
-        start = [[(zero, zero)] * count for _ in range(SWEEPS)]
+        def fill(i, carry):
+            r = i * 2
+            for c in range(count):
+                us = []
+                for k in range(2):
+                    g = (g_ref if c < groups else gs_ref)[l, pl.ds(r + k, 1), :]
+                    u = ek_row(l, c, r + k) * g
+                    u_ref[c, r + k] = u
+                    us.append(u)
+                store_lhs(c, r, us)
+            return carry
+
+        lax.fori_loop(0, hr // 2, fill, 0, unroll=2)
+        lax.fori_loop(0, hr // step, lambda i, x: (products(pl.multiple_of(i * step, step), step), x)[1], 0)
 
         def first(r, state):
-            gm = g_ref[l, pl.ds(r, 1), :]
-            gs = gs_ref[l, pl.ds(r, 1), :]
-            vals = [e_row(l, m, r) * gm for m in range(groups)] + [s_row(l, j, r) * gs for j in range(pairs)]
-            state, vals = sweep_all(state, vals, r)
+            state, vals = sweep_all(state, [u_ref[c, r] for c in range(count)], r)
             o = jnp.maximum(r - SWEEPS, 0)
             for m in range(groups):
                 p_ref[l * groups + m, o] = vals[m]
@@ -93,7 +140,17 @@
                 ps_ref[l * pairs + j, o] = vals[groups + j]
             return state
 
-        lax.fori_loop(0, hr, first, start)
+        lax.fori_loop(0, hr, first, start, unroll=UNROLL)
+
+        def refill(i, carry):
+            r = i * 2
+            for c in range(count):
+                p = p_ref.at[l * groups + c] if c < groups else ps_ref.at[l * pairs + c - groups]
+                store_lhs(c, r, [p[r], p[r + 1]])
+            return carry
+
+        lax.fori_loop(SWEEPS // 2, (hr - SWEEPS) // 2, refill, 0, unroll=2)
+        lax.fori_loop(0, hr // step, lambda i, x: (products(pl.multiple_of(i * step, step), step), x)[1], 0)
 
         def second(r, state):
             vals = [p_ref[l * groups + m, r] for m in range(groups)] + [ps_ref[l * pairs + j, r] for j in range(pairs)]
@@ -111,7 +168,7 @@
             yst_ref[l, o] = acc
             return state
 
-        lax.fori_loop(SWEEPS, hr - SWEEPS, second, start)
+        lax.fori_loop(SWEEPS, hr - SWEEPS, second, start, unroll=UNROLL)
     lane = lax.broadcasted_iota(jnp.int32, (rows, cols), 1)
     for l in range(levels):
         main = jnp.sum(ym_ref[l, W:W + rows], axis=1)
@@ -122,11 +179,12 @@
         y_ref[l] = jnp.where(lane < W, west, jnp.where(lane >= cols - W, east, main))
 
 
-def g_apply(e2, s2, gm, gs, dims):
+def g_apply(e2, s2, gm, gs, dd, wm, ws, dims):
     members, levels, rows, cols = dims
     hr = rows + 2 * W
     groups = members // 8
     pairs = groups // 2
+    count = groups + pairs
     vm = pl.BlockSpec(memory_space=pltpu.VMEM)
     f32 = jnp.float32
     return pl.pallas_call(
@@ -136,12 +194,62 @@
             jax.ShapeDtypeStruct((levels * pairs, hr, 8, cols), f32),
             jax.ShapeDtypeStruct((levels, rows, cols), f32),
         ),
-        in_specs=[vm] * 4,
+        in_specs=[vm] * 7,
         out_specs=(vm,) * 3,
-        scratch_shapes=[pltpu.VMEM((hr, cols), f32), pltpu.VMEM((hr, cols), f32),
-                        pltpu.VMEM((levels, hr, 8, cols), f32), pltpu.VMEM((levels, hr, 8, cols), f32)],
+        scratch_shapes=[pltpu.VMEM((hr, cols), f32),
+                        pltpu.VMEM((levels, hr, 8, cols), f32), pltpu.VMEM((levels, hr, 8, cols), f32),
+                        pltpu.VMEM((count, hr, 8, cols), f32),
+                        pltpu.VMEM((count, hr * 8, 2 * cols), jnp.bfloat16),
+                        pltpu.VMEM((count, hr * 8, SWEEPS * cols), f32)],
         compiler_params=pltpu.CompilerParams(vmem_limit_bytes=60000000),
-    )(e2, s2, gm, gs)
+    )(e2, s2, gm, gs, dd, wm, ws)
+
+
+def sum_kernel(x_ref, o_ref, mid_ref, ra_ref, rb_ref, sa, qa, sb, qb):
+    nx, ny = lax.axis_size("gx"), lax.axis_size("gy")
+    mx, my = lax.axis_index("gx"), lax.axis_index("gy")
+    bar = pltpu.get_barrier_semaphore()
+    for axis, n, me in (("gx", nx, mx), ("gy", ny, my)):
+        for k in range(1, n):
+            pl.semaphore_signal(bar, inc=1, device_id={axis: lax.rem(me + k, n)}, device_id_type=pl.DeviceIdType.MESH)
+    pl.semaphore_wait(bar, nx + ny - 2)
+
+    def stage(axis, n, me, src, land, ssem, rsem):
+        copies = []
+        for k in range(1, n):
+            copies.append(pltpu.make_async_remote_copy(
+                src_ref=src, dst_ref=land.at[k - 1], send_sem=ssem.at[k - 1], recv_sem=rsem.at[k - 1],
+                device_id={axis: lax.rem(me + k, n)}, device_id_type=pl.DeviceIdType.MESH))
+            copies[-1].start()
+        for c in copies:
+            c.wait_recv()
+        total = src[...]
+        for k in range(n - 1):
+            total = total + land[k]
+        return copies, total
+
+    ca, total = stage("gx", nx, mx, x_ref, ra_ref, sa, qa)
+    mid_ref[...] = total
+    cb, total = stage("gy", ny, my, mid_ref, rb_ref, sb, qb)
+    o_ref[...] = total
+    for c in ca + cb:
+        c.wait_send()
+
+
+def sum_all(x):
+    nx, ny = lax.axis_size("gx"), lax.axis_size("gy")
+    vm = pl.BlockSpec(memory_space=pltpu.VMEM)
+    dma = pltpu.SemaphoreType.DMA
+    return pl.pallas_call(
+        sum_kernel,
+        out_shape=jax.ShapeDtypeStruct(x.shape, x.dtype),
+        in_specs=[vm],
+        out_specs=vm,
+        scratch_shapes=[pltpu.VMEM(x.shape, x.dtype), pltpu.VMEM((nx - 1,) + x.shape, x.dtype),
+                        pltpu.VMEM((ny - 1,) + x.shape, x.dtype),
+                        dma((nx - 1,)), dma((nx - 1,)), dma((ny - 1,)), dma((ny - 1,))],
+        compiler_params=pltpu.CompilerParams(collective_id=0, has_side_effects=True),
+    )(x)
 
 
 def with_halo(cells, sides, width):
@@ -181,6 +289,11 @@
     )(flat(obs_cell), flat(obs_level), flat(innovation), flat(obs_weight))
     g0 = g0.reshape(levels, rows, cols)
     dd = dd.reshape(levels, rows, cols)
+    wm, ws = pl.pallas_call(
+        functools.partial(weight_kernel, cols=cols),
+        out_shape=(jax.ShapeDtypeStruct((2 * cols, SWEEPS * cols), jnp.bfloat16),) * 2,
+        out_specs=(vm, vm),
+    )()
     full = with_halo(ensemble.astype(f32), (("gy", 2), ("gx", 3)), W)
     e2 = full[..., W:W + cols].reshape(members * levels * hr, cols)
     st = strip_of(full, cols)
@@ -190,13 +303,13 @@
     def apply(g):
         gf = with_halo(g, (("gy", 1), ("gx", 2)), W)
         gs = strip_of(gf, cols)
-        return g_apply(e2, s2, gf[..., W:W + cols], jnp.concatenate([gs, gs], -1), ensemble.shape)
+        return g_apply(e2, s2, gf[..., W:W + cols], jnp.concatenate([gs, gs], -1), dd, wm, ws, ensemble.shape)
 
     p0, ps0, y0 = apply(g0)
     g1 = dd * y0
     p1, ps1, y1 = apply(g1)
-    sums = jnp.stack([jnp.sum(g0 * y0), jnp.sum(g1 * y0), jnp.sum(g1 * y1), jnp.sum(dd * y1 * y1)])
-    m = lax.psum(sums, ("gy", "gx"))
+    sums = jnp.stack([jnp.sum(v, axis=(0, 1)) for v in (g0 * y0, g1 * y0, g1 * y1, dd * y1 * y1)])
+    m = jnp.sum(sum_all(jnp.concatenate([sums, jnp.zeros_like(sums)])), axis=1)
     bn2 = m[0] + EPS
     c = (EPS - m[1]) / bn2
     alpha1 = (m[0] + m[1]) / bn2

time: 234 us -> 164 us (0.70)
  blocking collectives: 47.1 us -> 0 us
  Pallas kernels: 87.8 us -> 68.7 us
  other arithmetic: 19.9 us -> 17.3 us
    psum x1 -> x0, blocking collectives: 47.1 us -> none  [on_device(): m = lax.psum(sums, ('gy', 'gx'))]
    pallas_call x2, Pallas kernels: 85.7 us -> 46.3 us  [g_apply(): pl.pallas_call(functools.partial(g_kernel, members=members, levels=levels...]
    pallas_call x0 -> x2, Pallas kernels: none -> 20.2 us  [the longest x1 19 us: sum_all(): pl.pallas_call(sum_kernel, out_shape=jax.ShapeDtypeStruct(x.shape, x.dtyp...]
    another operation x1 -> x0, other arithmetic: 2.66 us -> none  [on_device(): jnp.stack([jnp.sum(g0 * y0), jnp.sum(g1 * y0), jnp.sum(g1 * y1), jnp.sum(...]
  transfers between devices with their start and end apart: 12 -> 12, of which waited for: 3 -> 2; matrix products, arithmetic and copies ran while one was open for 4% -> 5% of each run, Pallas kernels for 1% -> 2%
where the time goes in v2:
time: 164 us; the launch traced here: 163 us
  Pallas kernels  68.7 us (42%)
  starting transfers between devices  34.7 us (21%)
  local copies, waits for them, and re-layouts  32.3 us (20%)
  other arithmetic  17.3 us (11%)
  between operations  7.45 us (5%)
  waiting for transfers between devices  2.07 us (1%)
    pallas_call x2, Pallas kernels, g_apply(): pl.pallas_call(functools.partial(g_kernel, members=members, levels=levels...  46.3 us
    ppermute x6, starting transfers between devices, with_halo(): lax.ppermute(tail, axis, [(i, (i + 1) % count) for i in range(ends)])  26.9 us
    pallas_call x1, Pallas kernels, sum_all(): pl.pallas_call(sum_kernel, out_shape=jax.ShapeDtypeStruct(x.shape, x.dtyp...  19 us
    ppermute x6, starting transfers between devices, with_halo(): lax.ppermute(head, axis, [((i + 1) % count, i) for i in range(ends)])  7.76 us
    concatenate x1, other arithmetic, strip_of(): jnp.concatenate([full[..., :KEEP], pad, full[..., full.shape[-1] - KEEP:]...  6.61 us
    slice x5, local copies, waits for them, and re-layouts, with_halo(): lax.slice_in_dim(cells, cells.shape[dim] - width, cells.shape[dim], axis=...  6.45 us
    unnamed x32, local copies, waits for them, and re-layouts  4.08 us
  transfers between devices with their start and end apart: 12, of which 2 were waited for; matrix products, arithmetic and copies ran while one was open for 5% of the time, Pallas kernels for 2%

profile of v2, /device:TPU:0, one launch (start us, length us, event | category | flops | bytes accessed | tf_op | source)
XLA Modules:
  0.0 162.5 jit_solution(1861943563467473452)
XLA Ops:
  0.6 1.0 fusion.7
  1.6 1.3 collective-permute-start.1
  2.9 5.5 %collective-permute-start = (f32[32,2,8,128]{3,2,1,0:T(8,128)S(1)}, f32[32,2,8,128]{3,2,1,0:T(8,128)S(1)}, u32[]{:S(2)}, u32[]{:S(2)}) collective-permute-start(f32[32,2,8,128]{3,2,1,0:T(8,128)S(1)} %get-tuple-element.30), channel_id=1, source_target_pairs={{0,4},{4,8},{8,12},{12,16},{16,20},{20,24},{24,28},{1,5},{5,9},{9,... | collective-permute-start | bytes 786440 | tf_op jit(solution)/shard_map/ppermute | solution.py:263
  8.5 2.1 %shard_map.68 = (f32[128,128]{1,0:T(8,128)}, f32[128,128]{1,0:T(8,128)}) custom-call(s32[1,2048]{1,0:T(1,128)} %bitcast.45, s32[1,2048]{1,0:T(1,128)} %bitcast.46, f32[1,2048]{1,0:T(1,128)} %bitcast.47, f32[1,2048]{1,0:T(1,128)} %bitcast.48), custom_call_target="tpu_custom_call" | custom-call | tf_op jit(solution)/shard_map/pallas_call | solution.py:285
  10.6 0.8 fusion.11
  11.4 1.3 collective-permute-start.5
  12.7 5.4 %collective-permute-start.4 = (f32[2,8,128]{2,1,0:T(8,128)S(1)}, f32[2,8,128]{2,1,0:T(8,128)S(1)}, u32[]{:S(2)}, u32[]{:S(2)}) collective-permute-start(f32[2,8,128]{2,1,0:T(8,128)S(1)} %get-tuple-element.42), channel_id=1, source_target_pairs={{0,4},{4,8},{8,12},{12,16},{16,20},{20,24},{24,28},{1,5},{5,9},{9,... | collective-permute-start | bytes 24584 | tf_op jit(solution)/shard_map/ppermute | solution.py:263
  18.1 1.5 convert_element_type.3
  19.7 1.2 copy-done.1
  21.1 3.2 %fusion.5 = (f32[32,2,80,8]{3,2,1,0:T(8,128)}, f32[32,2,80,8]{3,2,1,0:T(8,128)}) fusion(f32[32,2,80,128]{3,2,1,0:T(8,128)S(1)} %pad_maximum_fusion.2), kind=kLoop, calls=%fused_computation.37 | loop fusion | bytes 655360 | tf_op jit(solution)/shard_map/slice | solution.py:260
  24.4 2.6 %copy.24 = f32[32,2,80,8]{2,3,1,0:T(8,128)S(1)} copy(f32[32,2,80,8]{3,2,1,0:T(8,128)} %get-tuple-element.27) | data formatting | bytes 327680 | tf_op jit(solution)/shard_map/slice | solution.py:259
  27.0 1.3 collective-permute-start.3
  28.3 1.4 copy.22
  29.7 3.0 %collective-permute-start.2 = (f32[32,2,80,8]{2,3,1,0:T(8,128)}, f32[32,2,80,8]{2,3,1,0:T(8,128)S(1)}, u32[]{:S(2)}, u32[]{:S(2)}) collective-permute-start(f32[32,2,80,8]{2,3,1,0:T(8,128)} %copy.22), channel_id=1, source_target_pairs={{0,1},{1,2},{2,3},{4,5},{5,6},{6,7},{8,9},{9,10},{10,11},{12,13},{... | collective-permute-start | bytes 491528 | tf_op jit(solution)/shard_map/ppermute | solution.py:263
  32.8 1.3 collective-permute-start.7
  34.1 3.7 %collective-permute-start.6 = (f32[2,80,8]{2,1,0:T(8,128)S(1)}, f32[2,80,8]{2,1,0:T(8,128)S(1)}, u32[]{:S(2)}, u32[]{:S(2)}) collective-permute-start(f32[2,80,8]{2,1,0:T(8,128)S(1)} %get-tuple-element.39), channel_id=1, source_target_pairs={{0,1},{1,2},{2,3},{4,5},{5,6},{6,7},{8,9},{9,10},{10,11},{12,13},{... | collective-permute-start | bytes 15368 | tf_op jit(solution)/shard_map/ppermute | solution.py:263
  37.8 1.2 shard_map.69
  39.1 0.9 pad_maximum_fusion.10
  40.0 0.9 concatenate.56.gs_ref
  40.9 3.3 %copy.25 = f32[32,2,80,8]{3,2,1,0:T(8,128)} copy(f32[32,2,80,8]{2,3,1,0:T(8,128)} %collective-permute-done.3) | data formatting | bytes 327680 | tf_op jit(solution)/shard_map/ppermute | solution.py:265
  44.1 2.3 %copy.23 = f32[32,2,80,8]{3,2,1,0:T(8,128)} copy(f32[32,2,80,8]{2,3,1,0:T(8,128)S(1)} %collective-permute-done.2) | data formatting | bytes 327680 | tf_op jit(solution)/shard_map/ppermute | solution.py:263
  46.7 1.4 copy-done.4
  48.1 6.6 %fusion.1 = f32[32,2,80,64]{3,2,1,0:T(8,128)} fusion(f32[32,2,80,8]{3,2,1,0:T(8,128)S(1)} %copy-done.4, f32[32,2,8,128]{3,2,1,0:T(8,128)S(1)} %collective-permute-done.1, f32[32,2,64,128]{3,2,1,0:T(8,128)S(1)} %copy-done.2, f32[32,2,8,128]{3,2,1,0:T(8,128)S(1)} %collective-permute-done, f32[32,2,80,8]{3,2,1,0:T(8,128)} %copy.23, ...), kind=kLoop, calls=%fused_computation.4 | loop fusion | flops 6225920 | bytes 4423680 | tf_op jit(solution)/shard_map/concatenate | solution.py:274
  54.7 3.3 %copy.26 = f32[2,2,8,2,80,64]{4,2,0,3,5,1:T(8,128)S(1)} copy(f32[2,2,8,2,80,64]{5,4,3,2,1,0:T(8,128)} %bitcast.34) | data formatting | bytes 2621440 | tf_op jit(solution)/shard_map/reshape | solution.py:300
  58.0 1.7 %reshape.50 = f32[2560,128]{0,1:T(8,128)S(1)} reshape(f32[2,2,8,80,2,64]{3,2,1,0,5,4:T(8,128)S(1)} %bitcast.36) | data formatting | bytes 2621440 | tf_op jit(solution)/shard_map/reshape | solution.py:301
  59.7 1.5 copy.27.s_ref
  61.2 23.2 %shard_map.70 = (f32[8,80,8,128]{3,2,1,0:T(8,128)}, f32[4,80,8,128]{3,2,1,0:T(8,128)}, f32[2,64,128]{2,1,0:T(8,128)}) custom-call(f32[5120,128]{1,0:T(8,128)} %bitcast.31, f32[2560,128]{1,0:T(8,128)} %copy.27.s_ref, f32[2,80,128]{2,1,0:T(8,128)} %copy-done.7, f32[2,80,128]{2,1,0:T(8,128)} %concatenate.56.gs_ref, f32[2,64,128]{2,1,0:T(8,128)} %bitcast.39, ...), custom_call_target="tpu_custom_call" | custom-call | tf_op jit(solution)/shard_map/pallas_call | solution.py:190
  84.4 0.8 mul.78
  85.2 1.3 collective-permute-start.9
  86.5 5.4 %collective-permute-start.8 = (f32[2,8,128]{2,1,0:T(8,128)S(1)}, f32[2,8,128]{2,1,0:T(8,128)S(1)}, u32[]{:S(2)}, u32[]{:S(2)}) collective-permute-start(f32[2,8,128]{2,1,0:T(8,128)S(1)} %get-tuple-element.40), channel_id=1, source_target_pairs={{0,4},{4,8},{8,12},{12,16},{16,20},{20,24},{24,28},{1,5},{5,9},{9,... | collective-permute-start | bytes 24584 | tf_op jit(solution)/shard_map/ppermute | solution.py:263
  92.0 1.3 collective-permute-done.8
  93.4 1.3 collective-permute-start.11
  94.7 3.8 %collective-permute-start.10 = (f32[2,80,8]{2,1,0:T(8,128)S(1)}, f32[2,80,8]{2,1,0:T(8,128)S(1)}, u32[]{:S(2)}, u32[]{:S(2)}) collective-permute-start(f32[2,80,8]{2,1,0:T(8,128)S(1)} %get-tuple-element.35), channel_id=1, source_target_pairs={{0,1},{1,2},{2,3},{4,5},{5,6},{6,7},{8,9},{9,10},{10,11},{12,13},{... | collective-permute-start | bytes 15368 | tf_op jit(solution)/shard_map/ppermute | solution.py:263
  98.6 0.7 collective-permute-done.10
  99.4 0.8 concatenate.60.gs_ref
  100.3 23.1 %shard_map.71 = (f32[8,80,8,128]{3,2,1,0:T(8,128)}, f32[4,80,8,128]{3,2,1,0:T(8,128)}, f32[2,64,128]{2,1,0:T(8,128)}) custom-call(f32[5120,128]{1,0:T(8,128)} %bitcast.32, f32[2560,128]{1,0:T(8,128)} %copy.27.s_ref, f32[2,80,128]{2,1,0:T(8,128)} %copy-done.8, f32[2,80,128]{2,1,0:T(8,128)} %concatenate.60.gs_ref, f32[2,64,128]{2,1,0:T(8,128)} %bitcast.40, ...), custom_call_target="tpu_custom_call" | custom-call | tf_op jit(solution)/shard_map/pallas_call | solution.py:190
  123.4 0.9 fusion.4
  124.3 0.6 concatenate.61.x_ref
  124.9 19.0 %shard_map.72 = f32[8,128]{1,0:T(8,128)} custom-call(f32[8,128]{1,0:T(8,128)} %concatenate.61.x_ref), custom_call_target="tpu_custom_call" | custom-call | tf_op jit(solution)/shard_map/pallas_call | solution.py:243
  143.9 0.8 reduce_sum.49
  144.7 0.6 fusion.12
  151.7 1.5 multiply_add_fusion.2
  153.2 1.3 multiply_add_fusion.1
  154.5 1.2 reshape.52
  155.7 0.6 copy.29
  156.3 1.1 fusion.6
  158.1 0.8 copy-done.6
  160.1 2.5 %pad_maximum_fusion.3 = f32[32,2,64,128]{3,2,1,0:T(8,128)} fusion(f32[32,2,64,8]{3,2,1,0:T(8,128)S(1)} %get-tuple-element.29, f32[32,2,64,112]{3,2,1,0:T(8,128)S(1)} %slice.141, f32[32,2,64,8]{3,2,1,0:T(8,128)S(1)} %get-tuple-element.28), kind=kLoop, calls=%fused_computation.14 | loop fusion | flops 1048576 | bytes 4194304 | tf_op jit(solution)/shard_map/concatenate | solution.py:328
  (52 shorter events, 2.7 us)
Async XLA Ops:
  1.6 18.0 %collective-permute-start.1 = (f32[32,2,8,128]{3,2,1,0:T(8,128)S(1)}, f32[32,2,8,128]{3,2,1,0:T(8,128)S(1)}, u32[]{:S(2)}, u32[]{:S(2)}) collective-permute-start(f32[32,2,8,128]{3,2,1,0:T(8,128)S(1)} %get-tuple-element.31), channel_id=1, source_target_pairs={{4,0},{8,4},{12,8},{16,12},{20,16},{24,20},{28,24},{5,1},{9,5},{13... | collective-permute-start | bytes 786440 | tf_op jit(solution)/shard_map/ppermute | solution.py:265
  2.9 16.7 %collective-permute-start = (f32[32,2,8,128]{3,2,1,0:T(8,128)S(1)}, f32[32,2,8,128]{3,2,1,0:T(8,128)S(1)}, u32[]{:S(2)}, u32[]{:S(2)}) collective-permute-start(f32[32,2,8,128]{3,2,1,0:T(8,128)S(1)} %get-tuple-element.30), channel_id=1, source_target_pairs={{0,4},{4,8},{8,12},{12,16},{16,20},{20,24},{24,28},{1,5},{5,9},{9,... | collective-permute-start | bytes 786440 | tf_op jit(solution)/shard_map/ppermute | solution.py:263
  10.6 9.0 %copy-start.12 = (f32[128,128]{1,0:T(8,128)S(1)}, f32[128,128]{1,0:T(8,128)}, u32[]{:S(2)}) copy-start(f32[128,128]{1,0:T(8,128)} %get-tuple-element.12) | copy-start | bytes 196612
  11.4 8.2 %collective-permute-start.5 = (f32[2,8,128]{2,1,0:T(8,128)S(1)}, f32[2,8,128]{2,1,0:T(8,128)S(1)}, u32[]{:S(2)}, u32[]{:S(2)}) collective-permute-start(f32[2,8,128]{2,1,0:T(8,128)S(1)} %get-tuple-element.43), channel_id=1, source_target_pairs={{4,0},{8,4},{12,8},{16,12},{20,16},{24,20},{28,24},{5,1},{9,5},{13... | collective-permute-start | bytes 24584 | tf_op jit(solution)/shard_map/ppermute | solution.py:265
  12.7 6.9 %collective-permute-start.4 = (f32[2,8,128]{2,1,0:T(8,128)S(1)}, f32[2,8,128]{2,1,0:T(8,128)S(1)}, u32[]{:S(2)}, u32[]{:S(2)}) collective-permute-start(f32[2,8,128]{2,1,0:T(8,128)S(1)} %get-tuple-element.42), channel_id=1, source_target_pairs={{0,4},{4,8},{8,12},{12,16},{16,20},{20,24},{24,28},{1,5},{5,9},{9,... | collective-permute-start | bytes 24584 | tf_op jit(solution)/shard_map/ppermute | solution.py:263
  19.6 1.3 copy-start.1
  19.6 1.5 copy-start.14
  19.6 1.5 copy-start.15
  19.6 13.1 %copy-start.7 = (f32[2,80,128]{2,1,0:T(8,128)}, f32[2,80,128]{2,1,0:T(8,128)S(1)}, u32[]{:S(2)}) copy-start(f32[2,80,128]{2,1,0:T(8,128)S(1)} %pad_maximum_fusion.16.g_ref) | copy-start | bytes 245764
  21.1 3.2 %copy-start = (f32[32,2,80,128]{3,2,1,0:T(8,128)}, f32[32,2,80,128]{3,2,1,0:T(8,128)S(1)}, u32[]{:S(2)}) copy-start(f32[32,2,80,128]{3,2,1,0:T(8,128)S(1)} %pad_maximum_fusion.2) | copy-start | bytes 7864324
  24.4 3.9 %copy-start.3 = (f32[32,2,80,8]{3,2,1,0:T(8,128)S(1)}, f32[32,2,80,8]{3,2,1,0:T(8,128)}, u32[]{:S(2)}) copy-start(f32[32,2,80,8]{3,2,1,0:T(8,128)} %get-tuple-element.26) | copy-start | bytes 491524
  27.0 13.9 %collective-permute-start.3 = (f32[32,2,80,8]{2,3,1,0:T(8,128)S(1)}, f32[32,2,80,8]{2,3,1,0:T(8,128)}, u32[]{:S(2)}, u32[]{:S(2)}) collective-permute-start(f32[32,2,80,8]{2,3,1,0:T(8,128)S(1)} %copy.24), channel_id=1, source_target_pairs={{1,0},{2,1},{3,2},{5,4},{6,5},{7,6},{9,8},{10,9},{11,10},{13,12},{... | collective-permute-start | bytes 491528 | tf_op jit(solution)/shard_map/ppermute | solution.py:265
  29.7 14.4 %collective-permute-start.2 = (f32[32,2,80,8]{2,3,1,0:T(8,128)}, f32[32,2,80,8]{2,3,1,0:T(8,128)S(1)}, u32[]{:S(2)}, u32[]{:S(2)}) collective-permute-start(f32[32,2,80,8]{2,3,1,0:T(8,128)} %copy.22), channel_id=1, source_target_pairs={{0,1},{1,2},{2,3},{4,5},{5,6},{6,7},{8,9},{9,10},{10,11},{12,13},{... | collective-permute-start | bytes 491528 | tf_op jit(solution)/shard_map/ppermute | solution.py:263
  32.8 6.2 %collective-permute-start.7 = (f32[2,80,8]{2,1,0:T(8,128)S(1)}, f32[2,80,8]{2,1,0:T(8,128)S(1)}, u32[]{:S(2)}, u32[]{:S(2)}) collective-permute-start(f32[2,80,8]{2,1,0:T(8,128)S(1)} %get-tuple-element.38), channel_id=1, source_target_pairs={{1,0},{2,1},{3,2},{5,4},{6,5},{7,6},{9,8},{10,9},{11,10},{13,12},{... | collective-permute-start | bytes 15368 | tf_op jit(solution)/shard_map/ppermute | solution.py:265
  34.1 4.9 %collective-permute-start.6 = (f32[2,80,8]{2,1,0:T(8,128)S(1)}, f32[2,80,8]{2,1,0:T(8,128)S(1)}, u32[]{:S(2)}, u32[]{:S(2)}) collective-permute-start(f32[2,80,8]{2,1,0:T(8,128)S(1)} %get-tuple-element.39), channel_id=1, source_target_pairs={{0,1},{1,2},{2,3},{4,5},{5,6},{6,7},{8,9},{9,10},{10,11},{12,13},{... | collective-permute-start | bytes 15368 | tf_op jit(solution)/shard_map/ppermute | solution.py:263
  44.1 2.6 %copy-start.2 = (f32[32,2,64,128]{3,2,1,0:T(8,128)S(1)}, f32[32,2,64,128]{3,2,1,0:T(8,128)}, u32[]{:S(2)}) copy-start(f32[32,2,64,128]{3,2,1,0:T(8,128)} %copy-done.1) | copy-start | bytes 6291460
  46.4 1.7 %copy-start.4 = (f32[32,2,80,8]{3,2,1,0:T(8,128)S(1)}, f32[32,2,80,8]{3,2,1,0:T(8,128)}, u32[]{:S(2)}) copy-start(f32[32,2,80,8]{3,2,1,0:T(8,128)} %copy.25) | copy-start | bytes 491524
  61.2 23.2 %copy-start.9 = (f32[128,128]{1,0:T(8,128)S(1)}, f32[128,128]{1,0:T(8,128)}, u32[]{:S(2)}) copy-start(f32[128,128]{1,0:T(8,128)} %get-tuple-element.13) | copy-start | bytes 196612
  85.2 6.7 %collective-permute-start.9 = (f32[2,8,128]{2,1,0:T(8,128)S(1)}, f32[2,8,128]{2,1,0:T(8,128)S(1)}, u32[]{:S(2)}, u32[]{:S(2)}) collective-permute-start(f32[2,8,128]{2,1,0:T(8,128)S(1)} %get-tuple-element.41), channel_id=1, source_target_pairs={{4,0},{8,4},{12,8},{16,12},{20,16},{24,20},{28,24},{5,1},{9,5},{13... | collective-permute-start | bytes 24584 | tf_op jit(solution)/shard_map/ppermute | solution.py:265
  86.5 6.8 %collective-permute-start.8 = (f32[2,8,128]{2,1,0:T(8,128)S(1)}, f32[2,8,128]{2,1,0:T(8,128)S(1)}, u32[]{:S(2)}, u32[]{:S(2)}) collective-permute-start(f32[2,8,128]{2,1,0:T(8,128)S(1)} %get-tuple-element.40), channel_id=1, source_target_pairs={{0,4},{4,8},{8,12},{12,16},{16,20},{20,24},{24,28},{1,5},{5,9},{9,... | collective-permute-start | bytes 24584 | tf_op jit(solution)/shard_map/ppermute | solution.py:263
  93.3 6.9 %copy-start.8 = (f32[2,80,128]{2,1,0:T(8,128)}, f32[2,80,128]{2,1,0:T(8,128)S(1)}, u32[]{:S(2)}) copy-start(f32[2,80,128]{2,1,0:T(8,128)S(1)} %pad_maximum_fusion.17.g_ref) | copy-start | bytes 245764
  93.4 5.1 %collective-permute-start.11 = (f32[2,80,8]{2,1,0:T(8,128)S(1)}, f32[2,80,8]{2,1,0:T(8,128)S(1)}, u32[]{:S(2)}, u32[]{:S(2)}) collective-permute-start(f32[2,80,8]{2,1,0:T(8,128)S(1)} %get-tuple-element.34), channel_id=1, source_target_pairs={{1,0},{2,1},{3,2},{5,4},{6,5},{7,6},{9,8},{10,9},{11,10},{13,12},{... | collective-permute-start | bytes 15368 | tf_op jit(solution)/shard_map/ppermute | solution.py:265
  94.7 4.6 %collective-permute-start.10 = (f32[2,80,8]{2,1,0:T(8,128)S(1)}, f32[2,80,8]{2,1,0:T(8,128)S(1)}, u32[]{:S(2)}, u32[]{:S(2)}) collective-permute-start(f32[2,80,8]{2,1,0:T(8,128)S(1)} %get-tuple-element.35), channel_id=1, source_target_pairs={{0,1},{1,2},{2,3},{4,5},{5,6},{6,7},{8,9},{9,10},{10,11},{12,13},{... | collective-permute-start | bytes 15368 | tf_op jit(solution)/shard_map/ppermute | solution.py:263
  99.4 24.0 %copy-start.10 = (f32[128,128]{1,0:T(8,128)S(1)}, f32[128,128]{1,0:T(8,128)}, u32[]{:S(2)}) copy-start(f32[128,128]{1,0:T(8,128)} %get-tuple-element.13) | copy-start | bytes 196612
  99.4 24.0 %copy-start.13 = (f32[2,64,128]{2,1,0:T(8,128)S(1)}, f32[2,64,128]{2,1,0:T(8,128)}, u32[]{:S(2)}) copy-start(f32[2,64,128]{2,1,0:T(8,128)} %get-tuple-element.16) | copy-start | bytes 196612
  100.3 52.9 %copy-start.11 = (f32[4,80,8,128]{3,2,1,0:T(8,128)S(1)}, f32[4,80,8,128]{3,2,1,0:T(8,128)}, u32[]{:S(2)}) copy-start(f32[4,80,8,128]{3,2,1,0:T(8,128)} %get-tuple-element.18) | copy-start | bytes 3932164
  156.3 1.7 %copy-start.5 = (f32[8,80,8,128]{3,2,1,0:T(8,128)S(1)}, f32[8,80,8,128]{3,2,1,0:T(8,128)}, u32[]{:S(2)}) copy-start(f32[8,80,8,128]{3,2,1,0:T(8,128)} %get-tuple-element.20) | copy-start | bytes 7864324
  156.3 2.5 %copy-start.6 = (f32[8,80,8,128]{3,2,1,0:T(8,128)S(1)}, f32[8,80,8,128]{3,2,1,0:T(8,128)}, u32[]{:S(2)}) copy-start(f32[8,80,8,128]{3,2,1,0:T(8,128)} %get-tuple-element.21) | copy-start | bytes 7864324

commit v3 on v2

--- a/solution.py
+++ b/solution.py
@@ -11,18 +11,17 @@
 KAPPA = 0.2
 EPS = 1e-06
 W = 2 * SWEEPS
-KEEP = 3 * W
 HALF = 64
 UNROLL = 4
 
 
-def scatter_kernel(cell_ref, level_ref, inn_ref, wt_ref, g_ref, d_ref, *, rows, cols):
+def scatter(cell_ref, level_ref, inn_ref, wt_ref, g_ref, d_ref):
+    levels, rows, cols = g_ref.shape
     cell = cell_ref[...]
     row = level_ref[...] * rows + cell // cols
     col = cell % cols
     n = cell.shape[1]
-    lr = g_ref.shape[0]
-    hot = jnp.where(lax.broadcasted_iota(jnp.int32, (lr, n), 0) == row, 1.0, 0.0).astype(jnp.bfloat16)
+    hot = jnp.where(lax.broadcasted_iota(jnp.int32, (levels * rows, n), 0) == row, 1.0, 0.0).astype(jnp.bfloat16)
     at = lax.broadcasted_iota(jnp.int32, (cols, n), 0) == col
     wt = wt_ref[...]
     for ref, v in ((g_ref, wt * inn_ref[...]), (d_ref, wt)):
@@ -33,7 +32,270 @@
             sel = jnp.where(at, part, 0.0).astype(jnp.bfloat16)
             term = lax.dot_general(hot, sel, (((1,), (1,)), ((), ())), preferred_element_type=jnp.float32)
             total = term if total is None else total + term
-        ref[...] = total
+        for l in range(levels):
+            ref[l] = total[l * rows:(l + 1) * rows]
+
+
+SIDES = [(-1, 0), (1, 0), (0, -1), (0, 1), (-1, -1), (-1, 1), (1, -1), (1, 1)]
+
+
+def peer(dy, dx):
+    ny, nx = lax.axis_size("gy"), lax.axis_size("gx")
+    return {"gy": lax.rem(lax.axis_index("gy") + dy + ny, ny), "gx": lax.rem(lax.axis_index("gx") + dx + nx, nx)}
+
+
+def meet():
+    bar = pltpu.get_barrier_semaphore()
+    for dy, dx in SIDES:
+        pl.semaphore_signal(bar, inc=1, device_id=peer(dy, dx), device_id_type=pl.DeviceIdType.MESH)
+    pl.semaphore_wait(bar, len(SIDES))
+
+
+def send_all(pairs, ssem, rsem):
+    copies = []
+    for n, ((dy, dx), (src, dst)) in enumerate(zip(SIDES, pairs)):
+        copies.append(pltpu.make_async_remote_copy(
+            src_ref=src, dst_ref=dst, send_sem=ssem.at[n], recv_sem=rsem.at[n],
+            device_id=peer(dy, dx), device_id_type=pl.DeviceIdType.MESH))
+        copies[-1].start()
+    return copies
+
+
+def pack_state(g_ref, pe_ref, pw_ref):
+    levels, rows, cols = g_ref.shape
+    block = lax.broadcasted_iota(jnp.int32, (8, cols), 1) // W
+    e = w = jnp.zeros((8, cols), jnp.float32)
+    per = rows // 8
+    for l in range(levels):
+        for t in range(per):
+            p = l * per + t
+            x = pltpu.roll(g_ref[l, t * 8:t * 8 + 8], (p * W + W) % cols, 1)
+            e = jnp.where(block == p, x, e)
+            w = jnp.where(block == (p + 1) % (cols // W), x, w)
+    pe_ref[...] = e
+    pw_ref[...] = w
+
+
+def unpack_state(g_ref, land_n, land_p, gm_ref, gs_ref):
+    levels, rows, cols = g_ref.shape
+    hr = rows + 2 * W
+    per = rows // 8
+    lane = lax.broadcasted_iota(jnp.int32, (8, cols), 1)
+    block = lane // W
+    gy, gx = lax.axis_index("gy"), lax.axis_index("gx")
+    c = strip_col(lane, cols) + gx * cols
+    cok = (lane % HALF < 6 * W) & (c >= 0) & (c < cols * lax.axis_size("gx"))
+    for l in range(levels):
+        for t in range(-1, per + 1):
+            if t < 0:
+                x, pe, pw, p = land_n[1, l], land_p[5], land_p[4], l * per + per - 1
+            elif t == per:
+                x, pe, pw, p = land_n[0, l], land_p[3], land_p[2], l * per
+            else:
+                x, pe, pw, p = g_ref[l, t * 8:t * 8 + 8], land_p[1], land_p[0], l * per + t
+            r = lax.broadcasted_iota(jnp.int32, (8, cols), 0) + gy * rows + t * 8
+            rok = (r >= 0) & (r < rows * lax.axis_size("gy"))
+            x = jnp.where(rok, x, 0.0)
+            z = jnp.where(block == p, pe, pw)
+            z1 = pltpu.roll(z, (cols - p * W) % cols, 1)
+            z2 = pltpu.roll(z, (cols - p * W + HALF) % cols, 1)
+            own = jnp.where(lane < HALF, pltpu.roll(x, 4 * W, 1), pltpu.roll(x, HALF + 4 * W, 1))
+            halo = jnp.where(lane < HALF, z1, z2)
+            gs = jnp.where(lane % HALF < 2 * W, halo, own)
+            at = slice((t + 1) * 8, (t + 2) * 8)
+            gm_ref[l, at] = x
+            gs_ref[l, at] = jnp.where(rok & cok, gs, 0.0)
+
+
+def state_pairs(g_ref, pe_ref, pw_ref, land_n, land_p):
+    rows = g_ref.shape[1]
+    return [(g_ref.at[:, 0:W], land_n.at[0]), (g_ref.at[:, rows - W:rows], land_n.at[1])] + [
+        (pw_ref if dx < 0 else pe_ref, land_p.at[n]) for n, (dy, dx) in enumerate(SIDES[2:])]
+
+
+def state_scratch(levels, cols):
+    f32 = jnp.float32
+    dma = pltpu.SemaphoreType.DMA
+    return [pltpu.VMEM((8, cols), f32), pltpu.VMEM((8, cols), f32), pltpu.VMEM((2, levels, W, cols), f32),
+            pltpu.VMEM((6, 8, cols), f32), dma((8,)), dma((8,))]
+
+
+def prep_kernel(ens_ref, cell_ref, level_ref, inn_ref, wt_ref, e_ref, s_ref, g_ref, d_ref, gm_ref, gs_ref,
+                ec_ref, pe_ref, pw_ref, en_ref, pee_ref, pew_ref, pc_ref, es, er,
+                gpe, gpw, gn, gp, ss, sr):
+    members, levels, rows, cols = ens_ref.shape
+    hr = rows + 2 * W
+    per = rows // 8
+    pairs = members // 16
+    lane = lax.broadcasted_iota(jnp.int32, (8, cols), 1)
+    block = lane // W
+    nb = cols // W
+
+    def convert(k, x):
+        for l in range(levels):
+            ec_ref[k * levels + l] = ens_ref[k, l].astype(jnp.float32)
+        return x
+
+    lax.fori_loop(0, members, convert, 0)
+
+    def pack(t, x):
+        at = pl.ds(pl.multiple_of(t * 8, 8), 8)
+        for l in range(levels):
+            for j in range(pairs):
+                e = w = jnp.zeros((8, cols), jnp.float32)
+                for b in range(2):
+                    for i in range(8):
+                        p = b * 8 + i
+                        x8 = pltpu.roll(ec_ref[(16 * j + p) * levels + l, at, :], (p * W + W) % cols, 1)
+                        e = jnp.where(block == p, x8, e)
+                        w = jnp.where(block == (p + 1) % nb, x8, w)
+                pe_ref[l * pairs + j, at, :] = e
+                pw_ref[l * pairs + j, at, :] = w
+        return x
+
+    lax.fori_loop(0, per, pack, 0)
+    meet()
+    top, bottom = slice(0, W), slice(rows - W, rows)
+    jobs = [(ec_ref.at[:, top], en_ref.at[0]), (ec_ref.at[:, bottom], en_ref.at[1]), (pw_ref, pew_ref), (pe_ref, pee_ref)]
+    for n, (dy, dx) in enumerate(SIDES[4:]):
+        src = pw_ref if dx < 0 else pe_ref
+        jobs.append((src.at[:, top if dy < 0 else bottom], pc_ref.at[n]))
+    ecopies = send_all(jobs, es, er)
+    scatter(cell_ref, level_ref, inn_ref, wt_ref, g_ref, d_ref)
+    pack_state(g_ref, gpe, gpw)
+    gcopies = send_all(state_pairs(g_ref, gpe, gpw, gn, gp), ss, sr)
+
+    def center(f, x):
+        e_ref[pl.ds(pl.multiple_of(f * hr + W, 8), rows), :] = ec_ref[f]
+        return x
+
+    lax.fori_loop(0, members * levels, center, 0)
+    for c in ecopies:
+        c.wait_recv()
+
+    def edges(f, x):
+        e_ref[pl.ds(pl.multiple_of(f * hr, 8), W), :] = en_ref[1, f]
+        e_ref[pl.ds(pl.multiple_of(f * hr + W + rows, 8), W), :] = en_ref[0, f]
+        return x
+
+    lax.fori_loop(0, members * levels, edges, 0)
+
+    def strip_tile(lj, i, l, j, row, pe, pw):
+        a = e_ref[pl.ds(pl.multiple_of(((16 * j + i) * levels + l) * hr + row, 8), 8), :]
+        b = e_ref[pl.ds(pl.multiple_of(((16 * j + 8 + i) * levels + l) * hr + row, 8), 8), :]
+        own = jnp.where(lane < HALF, pltpu.roll(a, 4 * W, 1), pltpu.roll(b, HALF + 4 * W, 1))
+        z = pltpu.roll(jnp.where(block % 8 == i, pe, pw), (cols - i * W) % cols, 1)
+        s_ref[pl.ds(pl.multiple_of((lj * 8 + i) * hr + row, 8), 8), :] = jnp.where(lane % HALF < 2 * W, z, own)
+
+    for l in range(levels):
+        for j in range(pairs):
+            lj = l * pairs + j
+
+            def mid(t, x):
+                at = pl.ds(pl.multiple_of(t * 8, 8), 8)
+                pe, pw = pee_ref[lj, at, :], pew_ref[lj, at, :]
+                for i in range(8):
+                    strip_tile(lj, i, l, j, W + t * 8, pe, pw)
+                return x
+
+            lax.fori_loop(0, per, mid, 0)
+            for i in range(8):
+                strip_tile(lj, i, l, j, 0, pc_ref[3, lj], pc_ref[2, lj])
+                strip_tile(lj, i, l, j, W + rows, pc_ref[1, lj], pc_ref[0, lj])
+    for c in gcopies:
+        c.wait_recv()
+    unpack_state(g_ref, gn, gp, gm_ref, gs_ref)
+    for c in ecopies + gcopies:
+        c.wait_send()
+
+
+def prep(ensemble, cell, level, inn, wt):
+    members, levels, rows, cols = ensemble.shape
+    hr = rows + 2 * W
+    f = members * levels
+    q = levels * (members // 16)
+    f32 = jnp.float32
+    vm = pl.BlockSpec(memory_space=pltpu.VMEM)
+    dma = pltpu.SemaphoreType.DMA
+    sds = lambda *s: jax.ShapeDtypeStruct(s, f32)
+    return pl.pallas_call(
+        prep_kernel,
+        out_shape=(sds(f * hr, cols), sds(q * 8 * hr, cols), sds(levels, rows, cols), sds(levels, rows, cols),
+                   sds(levels, hr, cols), sds(levels, hr, cols)),
+        in_specs=[vm] * 5,
+        out_specs=(vm,) * 6,
+        scratch_shapes=[pltpu.VMEM((f, rows, cols), f32), pltpu.VMEM((q, rows, cols), f32), pltpu.VMEM((q, rows, cols), f32),
+                        pltpu.VMEM((2, f, W, cols), f32), pltpu.VMEM((q, rows, cols), f32), pltpu.VMEM((q, rows, cols), f32),
+                        pltpu.VMEM((4, q, W, cols), f32), dma((8,)), dma((8,))] + state_scratch(levels, cols),
+        compiler_params=pltpu.CompilerParams(collective_id=1, has_side_effects=True, vmem_limit_bytes=60000000),
+    )(ensemble, cell, level, inn, wt)
+
+
+def next_kernel(y_ref, d_ref, gm_ref, gs_ref, g_ref, gpe, gpw, gn, gp, ss, sr):
+    g_ref[...] = d_ref[...] * y_ref[...]
+    pack_state(g_ref, gpe, gpw)
+    meet()
+    copies = send_all(state_pairs(g_ref, gpe, gpw, gn, gp), ss, sr)
+    for c in copies:
+        c.wait_recv()
+    unpack_state(g_ref, gn, gp, gm_ref, gs_ref)
+    for c in copies:
+        c.wait_send()
+
+
+def next_state(y, d):
+    levels, rows, cols = y.shape
+    vm = pl.BlockSpec(memory_space=pltpu.VMEM)
+    return pl.pallas_call(
+        next_kernel,
+        out_shape=(jax.ShapeDtypeStruct((levels, rows + 2 * W, cols), jnp.float32),) * 2,
+        in_specs=[vm] * 2,
+        out_specs=(vm,) * 2,
+        scratch_shapes=[pltpu.VMEM((levels, rows, cols), jnp.float32)] + state_scratch(levels, cols),
+        compiler_params=pltpu.CompilerParams(collective_id=2, has_side_effects=True),
+    )(y, d)
+
+
+def out_kernel(m_ref, p0_ref, s0_ref, p1_ref, s1_ref, y0_ref, y1_ref, c_ref, inc_ref):
+    levels, rows, cols = y0_ref.shape
+    groups = p0_ref.shape[0] // levels
+    pairs = groups // 2
+    m = jnp.sum(m_ref[...], axis=1, keepdims=True)
+    m = [m[k:k + 1] for k in range(4)]
+    bn2 = m[0] + EPS
+    c = (EPS - m[1]) / bn2
+    alpha1 = (m[0] + m[1]) / bn2
+    r2 = jnp.maximum((c * c * m[0] + 2.0 * c * m[1] + m[2]) / bn2, 0.0)
+    rho = (c * c * m[1] + 2.0 * c * m[2] + m[3]) / bn2
+    b2 = r2 + EPS
+    alpha2 = (r2 + rho) / b2
+    det = alpha1 * alpha2 - b2
+    ca = jnp.broadcast_to((alpha2 - c) / det, (8, cols))
+    cb = jnp.broadcast_to(-1.0 / det, (8, cols))
+    for l in range(levels):
+        for t in range(rows // 8):
+            at = slice(t * 8, t * 8 + 8)
+            inc_ref[l, at] = ca * y0_ref[l, at] + cb * y1_ref[l, at]
+    lane = lax.broadcasted_iota(jnp.int32, (8, cols), 1)
+    edge = (lane < W) | (lane >= cols - W)
+    for l in range(levels):
+        for j in range(pairs):
+            def row(r, x):
+                s = ca * s0_ref[l * pairs + j, W + r] + cb * s1_ref[l * pairs + j, W + r]
+                for b in range(2):
+                    g = l * groups + 2 * j + b
+                    main = ca * p0_ref[g, W + r] + cb * p1_ref[g, W + r]
+                    v = jnp.where(edge, pltpu.roll(s, (2 * cols - 4 * W - b * HALF) % cols, 1), main)
+                    c_ref[pl.ds(((2 * j + b) * 8 * levels + l) * rows + r, 8, stride=levels * rows), :] = v
+                return x
+
+            lax.fori_loop(0, rows, row, 0, unroll=8)
+
+
+def strip_col(lane, cols):
+    lane = lane % HALF
+    return jnp.where(lane < W, lane - W, jnp.where(lane < 2 * W, lane - W + cols,
+                     jnp.where(lane < 4 * W, lane - 4 * W + cols, lane - 4 * W)))
 
 
 def weight_kernel(wm_ref, ws_ref, *, cols):
@@ -43,13 +305,13 @@
     gx = lax.axis_index("gx")
 
     def real(lane):
-        lane = lane % HALF
-        west = lane < KEEP
-        c = jnp.where(west, lane - W, lane - HALF // 2 + cols - 2 * W) + gx * cols
-        inside = west | ((lane >= HALF // 2) & (lane < HALF // 2 + KEEP))
-        return inside & (c >= 0) & (c < cols * lax.axis_size("gx"))
-
-    for ref, ok in ((wm_ref, near), (ws_ref, near & real(i) & real(j))):
+        c = strip_col(lane, cols) + gx * cols
+        return (lane % HALF < 6 * W) & (c >= 0) & (c < cols * lax.axis_size("gx"))
+
+    si, sj = strip_col(i, cols), strip_col(j, cols)
+    same = ((i < HALF) == (j < HALF)) & (jnp.abs(si - sj) <= 1)
+
+    for ref, ok in ((wm_ref, near), (ws_ref, same & real(i) & real(j))):
         one = jnp.where(ok, 1.0, 0.0).astype(jnp.bfloat16)
         power = one
         for s in range(1, SWEEPS + 1):
@@ -60,7 +322,7 @@
             ref[cols:2 * cols, (s - 1) * cols:s * cols] = scaled
 
 
-def g_kernel(e_ref, s_ref, g_ref, gs_ref, d_ref, wm_ref, ws_ref, p_ref, ps_ref, y_ref, km_ref, ym_ref, yst_ref,
+def g_kernel(e_ref, s_ref, g_ref, gs_ref, wm_ref, ws_ref, p_ref, ps_ref, y_ref, km_ref, ym_ref, yst_ref,
              u_ref, lhs_ref, f_ref, *, members, levels, rows, cols):
     hr = rows + 2 * W
     groups = members // 8
@@ -174,12 +436,10 @@
         main = jnp.sum(ym_ref[l, W:W + rows], axis=1)
         st = jnp.sum(yst_ref[l, W:W + rows], axis=1)
         st = st + pltpu.roll(st, HALF, 1)
-        west = pltpu.roll(st, cols - W, 1)
-        east = pltpu.roll(st, cols - W - (HALF // 2 + W), 1)
-        y_ref[l] = jnp.where(lane < W, west, jnp.where(lane >= cols - W, east, main))
-
-
-def g_apply(e2, s2, gm, gs, dd, wm, ws, dims):
+        y_ref[l] = jnp.where((lane < W) | (lane >= cols - W), pltpu.roll(st, cols - 4 * W, 1), main)
+
+
+def g_apply(e2, s2, gm, gs, wm, ws, dims):
     members, levels, rows, cols = dims
     hr = rows + 2 * W
     groups = members // 8
@@ -194,7 +454,7 @@
             jax.ShapeDtypeStruct((levels * pairs, hr, 8, cols), f32),
             jax.ShapeDtypeStruct((levels, rows, cols), f32),
         ),
-        in_specs=[vm] * 7,
+        in_specs=[vm] * 6,
         out_specs=(vm,) * 3,
         scratch_shapes=[pltpu.VMEM((hr, cols), f32),
                         pltpu.VMEM((levels, hr, 8, cols), f32), pltpu.VMEM((levels, hr, 8, cols), f32),
@@ -202,7 +462,7 @@
                         pltpu.VMEM((count, hr * 8, 2 * cols), jnp.bfloat16),
                         pltpu.VMEM((count, hr * 8, SWEEPS * cols), f32)],
         compiler_params=pltpu.CompilerParams(vmem_limit_bytes=60000000),
-    )(e2, s2, gm, gs, dd, wm, ws)
+    )(e2, s2, gm, gs, wm, ws)
 
 
 def sum_kernel(x_ref, o_ref, mid_ref, ra_ref, rb_ref, sa, qa, sb, qb):
@@ -252,82 +512,30 @@
     )(x)
 
 
-def with_halo(cells, sides, width):
-    for axis, dim in sides:
-        count = lax.axis_size(axis)
-        ends = count - 1
-        head = lax.slice_in_dim(cells, 0, width, axis=dim)
-        tail = lax.slice_in_dim(cells, cells.shape[dim] - width, cells.shape[dim], axis=dim)
-        cells = jnp.concatenate(
-            [
-                lax.ppermute(tail, axis, [(i, (i + 1) % count) for i in range(ends)]),
-                cells,
-                lax.ppermute(head, axis, [((i + 1) % count, i) for i in range(ends)]),
-            ],
-            axis=dim,
-        )
-    return cells
-
-
-def strip_of(full, cols):
-    pad = jnp.zeros(full.shape[:-1] + (HALF // 2 - KEEP,), full.dtype)
-    return jnp.concatenate([full[..., :KEEP], pad, full[..., full.shape[-1] - KEEP:], pad], axis=-1)
-
-
 def on_device(ensemble, obs_cell, obs_level, innovation, obs_weight):
     members, levels, rows, cols = ensemble.shape
-    groups = members // 8
-    pairs = groups // 2
-    hr = rows + 2 * W
     f32 = jnp.float32
     vm = pl.BlockSpec(memory_space=pltpu.VMEM)
     flat = lambda a: a.reshape(1, -1)
-    g0, dd = pl.pallas_call(
-        functools.partial(scatter_kernel, rows=rows, cols=cols),
-        out_shape=(jax.ShapeDtypeStruct((levels * rows, cols), f32),) * 2,
-        in_specs=[vm] * 4, out_specs=(vm, vm),
-    )(flat(obs_cell), flat(obs_level), flat(innovation), flat(obs_weight))
-    g0 = g0.reshape(levels, rows, cols)
-    dd = dd.reshape(levels, rows, cols)
+    e2, s2, g0, dd, gm, gs = prep(ensemble, flat(obs_cell), flat(obs_level), flat(innovation), flat(obs_weight))
     wm, ws = pl.pallas_call(
         functools.partial(weight_kernel, cols=cols),
         out_shape=(jax.ShapeDtypeStruct((2 * cols, SWEEPS * cols), jnp.bfloat16),) * 2,
         out_specs=(vm, vm),
     )()
-    full = with_halo(ensemble.astype(f32), (("gy", 2), ("gx", 3)), W)
-    e2 = full[..., W:W + cols].reshape(members * levels * hr, cols)
-    st = strip_of(full, cols)
-    st = st.reshape(pairs, 2, 8, levels, hr, HALF).transpose(3, 0, 2, 4, 1, 5)
-    s2 = st.reshape(levels * pairs * 8 * hr, cols)
-
-    def apply(g):
-        gf = with_halo(g, (("gy", 1), ("gx", 2)), W)
-        gs = strip_of(gf, cols)
-        return g_apply(e2, s2, gf[..., W:W + cols], jnp.concatenate([gs, gs], -1), dd, wm, ws, ensemble.shape)
-
-    p0, ps0, y0 = apply(g0)
-    g1 = dd * y0
-    p1, ps1, y1 = apply(g1)
-    sums = jnp.stack([jnp.sum(v, axis=(0, 1)) for v in (g0 * y0, g1 * y0, g1 * y1, dd * y1 * y1)])
-    m = jnp.sum(sum_all(jnp.concatenate([sums, jnp.zeros_like(sums)])), axis=1)
-    bn2 = m[0] + EPS
-    c = (EPS - m[1]) / bn2
-    alpha1 = (m[0] + m[1]) / bn2
-    r2 = jnp.maximum((c * c * m[0] + 2.0 * c * m[1] + m[2]) / bn2, 0.0)
-    rho = (c * c * m[1] + 2.0 * c * m[2] + m[3]) / bn2
-    b2 = r2 + EPS
-    alpha2 = (r2 + rho) / b2
-    det = alpha1 * alpha2 - b2
-    ca = (alpha2 - c) / det
-    cb = -1.0 / det
-
-    pm = ca * p0[:, W:W + rows] + cb * p1[:, W:W + rows]
-    ps = ca * ps0[:, W:W + rows] + cb * ps1[:, W:W + rows]
-    pm = pm.reshape(levels, pairs, 2, rows, 8, cols).transpose(1, 2, 4, 0, 3, 5).reshape(members, levels, rows, cols)
-    ps = ps.reshape(levels, pairs, rows, 8, 2, HALF).transpose(1, 4, 3, 0, 2, 5).reshape(members, levels, rows, HALF)
-    control = jnp.concatenate([ps[..., W:2 * W], pm[..., W:cols - W], ps[..., HALF // 2 + W:HALF // 2 + 2 * W]], -1)
-    increment = ca * y0 + cb * y1
-    return (control, increment)
+    p0, ps0, y0 = g_apply(e2, s2, gm, gs, wm, ws, ensemble.shape)
+    gm1, gs1 = next_state(y0, dd)
+    p1, ps1, y1 = g_apply(e2, s2, gm1, gs1, wm, ws, ensemble.shape)
+    sums = jnp.stack([jnp.sum(v, axis=(0, 1)) for v in (g0 * y0, dd * y0 * y0, dd * y0 * y1, dd * y1 * y1)])
+    m = sum_all(jnp.concatenate([sums, jnp.zeros_like(sums)]))
+    control, increment = pl.pallas_call(
+        out_kernel,
+        out_shape=(jax.ShapeDtypeStruct((members * levels * rows, cols), f32), jax.ShapeDtypeStruct((levels, rows, cols), f32)),
+        in_specs=[vm] * 7,
+        out_specs=(vm, vm),
+        compiler_params=pltpu.CompilerParams(vmem_limit_bytes=60000000),
+    )(m, p0, ps0, p1, ps1, y0, y1)
+    return (control.reshape(members, levels, rows, cols), increment)
 
 
 def solution(mesh):

time: 164 us -> 106 us (0.65)
  Pallas kernels: 68.7 us -> 104 us
  starting transfers between devices: 34.7 us -> 0 us
  local copies, waits for them, and re-layouts: 32.3 us -> 0.62 us
  other arithmetic: 17.3 us -> 0.88 us
  between operations: 7.45 us -> 0.69 us
  waiting for transfers between devices: 2.07 us -> 0 us
    pallas_call x1 -> x3, Pallas kernels: 2.13 us -> 45.6 us  [the longest x1 27.9 us: prep(): pl.pallas_call(prep_kernel, out_shape=(sds(f * hr, cols), sds(q * 8 * hr,...]
    ppermute x12 -> x0, starting transfers between devices: 34.7 us -> none  [the longest x6 26.9 us: with_halo(): lax.ppermute(tail, axis, [(i, (i + 1) % count) for i in range(ends)])]
    slice x11 -> x0, local copies, waits for them, and re-layouts: 11.6 us -> none  [the longest x5 6.45 us: with_halo(): lax.slice_in_dim(cells, cells.shape[dim] - width, cells.shape[dim], axis=...]
    concatenate x7 -> x0, other arithmetic: 10.3 us -> none  [the longest x1 6.61 us: strip_of(): jnp.concatenate([full[..., :KEEP], pad, full[..., full.shape[-1] - KEEP:]...]
    pallas_call x1, Pallas kernels: 19 us -> 10.9 us  [sum_all(): pl.pallas_call(sum_kernel, out_shape=jax.ShapeDtypeStruct(x.shape, x.dtyp...]
    reshape x4 -> x0, local copies, waits for them, and re-layouts: 7.6 us -> none  [the longest x1 3.25 us: on_device(): st = st.reshape(pairs, 2, 8, levels, hr, HALF).transpose(3, 0, 2, 4, 1, 5)]
    ppermute x2 -> x0, local copies, waits for them, and re-layouts: 5.51 us -> none  [the longest x1 3.26 us: with_halo(): lax.ppermute(head, axis, [((i + 1) % count, i) for i in range(ends)])]
    unnamed x32 -> x6, local copies, waits for them, and re-layouts: 4.08 us -> 0.01 us
  transfers between devices with their start and end apart: 12 -> 0, of which waited for: 2 -> 0; matrix products, arithmetic and copies ran while one was open for 5% -> 0% of each run, Pallas kernels for 2% -> 0%
where the time goes in v3:
time: 106 us
  Pallas kernels  104 us (98%)
    pallas_call x2, Pallas kernels, g_apply(): pl.pallas_call(functools.partial(g_kernel, members=members, levels=levels...  46 us
    pallas_call x1, Pallas kernels, prep(): pl.pallas_call(prep_kernel, out_shape=(sds(f * hr, cols), sds(q * 8 * hr,...  27.9 us
    pallas_call x1, Pallas kernels, sum_all(): pl.pallas_call(sum_kernel, out_shape=jax.ShapeDtypeStruct(x.shape, x.dtyp...  10.9 us
    pallas_call x1, Pallas kernels, next_state(): pl.pallas_call(next_kernel, out_shape=(jax.ShapeDtypeStruct((levels, rows...  9.15 us
    pallas_call x1, Pallas kernels, on_device(): pl.pallas_call(out_kernel, out_shape=(jax.ShapeDtypeStruct((members * lev...  8.61 us

profile of v3, /device:TPU:0, one launch (start us, length us, event | category | flops | bytes accessed | tf_op | source)
XLA Modules:
  0.0 106.0 jit_solution(3596002346970993995)
XLA Ops:
  0.6 27.9 %shard_map.68 = (f32[5120,128]{1,0:T(8,128)}, f32[2560,128]{1,0:T(8,128)}, f32[2,64,128]{2,1,0:T(8,128)}, f32[2,64,128]{2,1,0:T(8,128)}, f32[2,80,128]{2,1,0:T(8,128)}, /*index=5*/f32[2,80,128]{2,1,0:T(8,128)}) custom-call(bf16[32,2,64,128]{3,2,1,0:T(8,128)(2,1)} %ens_ref.1, s32[1,2048]{1,0:T(1,128)} %bitcast.9, s32[1,2048]{1,0:T(1,128)} %bitcast.10, ...), custom_call_target="tpu_custom_call" | custom-call | tf_op jit(solution)/shard_map/pallas_call | solution.py:221
  28.5 1.2 %shard_map.69 = (bf16[256,512]{1,0:T(8,128)(2,1)}, bf16[256,512]{1,0:T(8,128)(2,1)}) custom-call(), custom_call_target="tpu_custom_call" | custom-call | tf_op jit(solution)/shard_map/pallas_call | solution.py:521
  29.8 23.0 %shard_map.70 = (f32[8,80,8,128]{3,2,1,0:T(8,128)}, f32[4,80,8,128]{3,2,1,0:T(8,128)}, f32[2,64,128]{2,1,0:T(8,128)}) custom-call(f32[5120,128]{1,0:T(8,128)} %get-tuple-element.21.e_ref, f32[2560,128]{1,0:T(8,128)} %get-tuple-element.22.s_ref, f32[2,80,128]{2,1,0:T(8,128)} %get-tuple-element.23.g_ref, f32[2,80,128]{2,1,0:T(8,128)} %get-tuple-element.24.gs_ref, ...), custom_call_target="tpu_custom_call" | custom-call | tf_op jit(solution)/shard_map/pallas_call | solution.py:450
  52.7 9.2 %shard_map.71 = (f32[2,80,128]{2,1,0:T(8,128)}, f32[2,80,128]{2,1,0:T(8,128)}) custom-call(f32[2,64,128]{2,1,0:T(8,128)} %get-tuple-element.27.y_ref.y0_ref, f32[2,64,128]{2,1,0:T(8,128)} %get-tuple-element.28.d_ref), custom_call_target="tpu_custom_call" | custom-call | tf_op jit(solution)/shard_map/pallas_call | solution.py:249
  61.9 0.0 copy-start
  61.9 0.0 copy-start.1
  61.9 0.0 copy-start.2
  61.9 23.0 %shard_map.72 = (f32[8,80,8,128]{3,2,1,0:T(8,128)}, f32[4,80,8,128]{3,2,1,0:T(8,128)}, f32[2,64,128]{2,1,0:T(8,128)}) custom-call(f32[5120,128]{1,0:T(8,128)} %get-tuple-element.21.e_ref, f32[2560,128]{1,0:T(8,128)} %get-tuple-element.22.s_ref, f32[2,80,128]{2,1,0:T(8,128)} %get-tuple-element.29.g_ref, f32[2,80,128]{2,1,0:T(8,128)} %get-tuple-element.30.gs_ref, ...), custom_call_target="tpu_custom_call" | custom-call | tf_op jit(solution)/shard_map/pallas_call | solution.py:450
  84.9 0.0 copy-done
  84.9 0.0 copy-done.1
  84.9 0.0 copy-done.2
  84.9 0.9 fusion
  85.8 0.6 concatenate.3.x_ref
  86.4 10.9 %shard_map.73.m_ref = f32[8,128]{1,0:T(8,128)} custom-call(f32[8,128]{1,0:T(8,128)} %concatenate.3.x_ref), custom_call_target="tpu_custom_call" | custom-call | tf_op jit(solution)/shard_map/pallas_call | solution.py:503
  97.4 8.6 %shard_map.74 = (f32[4096,128]{1,0:T(8,128)}, f32[2,64,128]{2,1,0:T(8,128)}) custom-call(f32[8,128]{1,0:T(8,128)} %shard_map.73.m_ref, f32[8,80,8,128]{3,2,1,0:T(8,128)} %get-tuple-element.32.p0_ref, f32[4,80,8,128]{3,2,1,0:T(8,128)} %get-tuple-element.33.s0_ref, f32[8,80,8,128]{3,2,1,0:T(8,128)} %get-tuple-element.34.p1_ref, ...), custom_call_target="tpu_custom_call" | custom-call | tf_op jit(solution)/shard_map/pallas_call | solution.py:531
  (1 shorter events, 0.0 us)
Async XLA Ops:
  61.9 23.1 %copy-start = (f32[2,64,128]{2,1,0:T(8,128)S(1)}, f32[2,64,128]{2,1,0:T(8,128)}, u32[]{:S(2)}) copy-start(f32[2,64,128]{2,1,0:T(8,128)} %get-tuple-element.27.y_ref.y0_ref) | copy-start | bytes 196612
  61.9 23.1 %copy-start.1 = (f32[2,64,128]{2,1,0:T(8,128)S(1)}, f32[2,64,128]{2,1,0:T(8,128)}, u32[]{:S(2)}) copy-start(f32[2,64,128]{2,1,0:T(8,128)} %get-tuple-element.28.d_ref) | copy-start | bytes 196612
  61.9 23.1 %copy-start.2 = (f32[2,64,128]{2,1,0:T(8,128)S(1)}, f32[2,64,128]{2,1,0:T(8,128)}, u32[]{:S(2)}) copy-start(f32[2,64,128]{2,1,0:T(8,128)} %get-tuple-element.20) | copy-start | bytes 196612

commit v4 on v3

--- a/solution.py
+++ b/solution.py
@@ -48,7 +48,13 @@
     bar = pltpu.get_barrier_semaphore()
     for dy, dx in SIDES:
         pl.semaphore_signal(bar, inc=1, device_id=peer(dy, dx), device_id_type=pl.DeviceIdType.MESH)
-    pl.semaphore_wait(bar, len(SIDES))
+    total = len(SIDES)
+    for axis in ("gx", "gy"):
+        n, me = lax.axis_size(axis), lax.axis_index(axis)
+        total += n - 1
+        for k in range(1, n):
+            pl.semaphore_signal(bar, inc=1, device_id={axis: lax.rem(me + k, n)}, device_id_type=pl.DeviceIdType.MESH)
+    pl.semaphore_wait(bar, total)
 
 
 def send_all(pairs, ssem, rsem):
@@ -121,7 +127,7 @@
 
 
 def prep_kernel(ens_ref, cell_ref, level_ref, inn_ref, wt_ref, e_ref, s_ref, g_ref, d_ref, gm_ref, gs_ref,
-                ec_ref, pe_ref, pw_ref, en_ref, pee_ref, pew_ref, pc_ref, es, er,
+                wm_ref, ws_ref, ec_ref, pe_ref, pw_ref, en_ref, pee_ref, pew_ref, pc_ref, es, er,
                 gpe, gpw, gn, gp, ss, sr):
     members, levels, rows, cols = ens_ref.shape
     hr = rows + 2 * W
@@ -170,6 +176,7 @@
         return x
 
     lax.fori_loop(0, members * levels, center, 0)
+    weight_kernel(wm_ref, ws_ref, cols=cols)
     for c in ecopies:
         c.wait_recv()
 
@@ -209,51 +216,15 @@
         c.wait_send()
 
 
-def prep(ensemble, cell, level, inn, wt):
-    members, levels, rows, cols = ensemble.shape
-    hr = rows + 2 * W
-    f = members * levels
-    q = levels * (members // 16)
-    f32 = jnp.float32
-    vm = pl.BlockSpec(memory_space=pltpu.VMEM)
-    dma = pltpu.SemaphoreType.DMA
-    sds = lambda *s: jax.ShapeDtypeStruct(s, f32)
-    return pl.pallas_call(
-        prep_kernel,
-        out_shape=(sds(f * hr, cols), sds(q * 8 * hr, cols), sds(levels, rows, cols), sds(levels, rows, cols),
-                   sds(levels, hr, cols), sds(levels, hr, cols)),
-        in_specs=[vm] * 5,
-        out_specs=(vm,) * 6,
-        scratch_shapes=[pltpu.VMEM((f, rows, cols), f32), pltpu.VMEM((q, rows, cols), f32), pltpu.VMEM((q, rows, cols), f32),
-                        pltpu.VMEM((2, f, W, cols), f32), pltpu.VMEM((q, rows, cols), f32), pltpu.VMEM((q, rows, cols), f32),
-                        pltpu.VMEM((4, q, W, cols), f32), dma((8,)), dma((8,))] + state_scratch(levels, cols),
-        compiler_params=pltpu.CompilerParams(collective_id=1, has_side_effects=True, vmem_limit_bytes=60000000),
-    )(ensemble, cell, level, inn, wt)
-
-
 def next_kernel(y_ref, d_ref, gm_ref, gs_ref, g_ref, gpe, gpw, gn, gp, ss, sr):
     g_ref[...] = d_ref[...] * y_ref[...]
     pack_state(g_ref, gpe, gpw)
-    meet()
     copies = send_all(state_pairs(g_ref, gpe, gpw, gn, gp), ss, sr)
     for c in copies:
         c.wait_recv()
     unpack_state(g_ref, gn, gp, gm_ref, gs_ref)
     for c in copies:
         c.wait_send()
-
-
-def next_state(y, d):
-    levels, rows, cols = y.shape
-    vm = pl.BlockSpec(memory_space=pltpu.VMEM)
-    return pl.pallas_call(
-        next_kernel,
-        out_shape=(jax.ShapeDtypeStruct((levels, rows + 2 * W, cols), jnp.float32),) * 2,
-        in_specs=[vm] * 2,
-        out_specs=(vm,) * 2,
-        scratch_shapes=[pltpu.VMEM((levels, rows, cols), jnp.float32)] + state_scratch(levels, cols),
-        compiler_params=pltpu.CompilerParams(collective_id=2, has_side_effects=True),
-    )(y, d)
 
 
 def out_kernel(m_ref, p0_ref, s0_ref, p1_ref, s1_ref, y0_ref, y1_ref, c_ref, inc_ref):
@@ -369,7 +340,7 @@
 
     zero = km_ref[0:8, :] * 0.0
     start = [[(zero, zero)] * count for _ in range(SWEEPS)]
-    step = 16
+    step = hr
 
     def store_lhs(c, r, us):
         his, los = zip(*[split(c, r, u) for u in us])
@@ -391,7 +362,7 @@
             return carry
 
         lax.fori_loop(0, hr // 2, fill, 0, unroll=2)
-        lax.fori_loop(0, hr // step, lambda i, x: (products(pl.multiple_of(i * step, step), step), x)[1], 0)
+        products(0, step)
 
         def first(r, state):
             state, vals = sweep_all(state, [u_ref[c, r] for c in range(count)], r)
@@ -412,7 +383,7 @@
             return carry
 
         lax.fori_loop(SWEEPS // 2, (hr - SWEEPS) // 2, refill, 0, unroll=2)
-        lax.fori_loop(0, hr // step, lambda i, x: (products(pl.multiple_of(i * step, step), step), x)[1], 0)
+        products(0, step)
 
         def second(r, state):
             vals = [p_ref[l * groups + m, r] for m in range(groups)] + [ps_ref[l * pairs + j, r] for j in range(pairs)]
@@ -439,41 +410,9 @@
         y_ref[l] = jnp.where((lane < W) | (lane >= cols - W), pltpu.roll(st, cols - 4 * W, 1), main)
 
 
-def g_apply(e2, s2, gm, gs, wm, ws, dims):
-    members, levels, rows, cols = dims
-    hr = rows + 2 * W
-    groups = members // 8
-    pairs = groups // 2
-    count = groups + pairs
-    vm = pl.BlockSpec(memory_space=pltpu.VMEM)
-    f32 = jnp.float32
-    return pl.pallas_call(
-        functools.partial(g_kernel, members=members, levels=levels, rows=rows, cols=cols),
-        out_shape=(
-            jax.ShapeDtypeStruct((levels * groups, hr, 8, cols), f32),
-            jax.ShapeDtypeStruct((levels * pairs, hr, 8, cols), f32),
-            jax.ShapeDtypeStruct((levels, rows, cols), f32),
-        ),
-        in_specs=[vm] * 6,
-        out_specs=(vm,) * 3,
-        scratch_shapes=[pltpu.VMEM((hr, cols), f32),
-                        pltpu.VMEM((levels, hr, 8, cols), f32), pltpu.VMEM((levels, hr, 8, cols), f32),
-                        pltpu.VMEM((count, hr, 8, cols), f32),
-                        pltpu.VMEM((count, hr * 8, 2 * cols), jnp.bfloat16),
-                        pltpu.VMEM((count, hr * 8, SWEEPS * cols), f32)],
-        compiler_params=pltpu.CompilerParams(vmem_limit_bytes=60000000),
-    )(e2, s2, gm, gs, wm, ws)
-
-
 def sum_kernel(x_ref, o_ref, mid_ref, ra_ref, rb_ref, sa, qa, sb, qb):
     nx, ny = lax.axis_size("gx"), lax.axis_size("gy")
     mx, my = lax.axis_index("gx"), lax.axis_index("gy")
-    bar = pltpu.get_barrier_semaphore()
-    for axis, n, me in (("gx", nx, mx), ("gy", ny, my)):
-        for k in range(1, n):
-            pl.semaphore_signal(bar, inc=1, device_id={axis: lax.rem(me + k, n)}, device_id_type=pl.DeviceIdType.MESH)
-    pl.semaphore_wait(bar, nx + ny - 2)
-
     def stage(axis, n, me, src, land, ssem, rsem):
         copies = []
         for k in range(1, n):
@@ -496,45 +435,57 @@
         c.wait_send()
 
 
-def sum_all(x):
+def whole_kernel(ens_ref, cell_ref, level_ref, inn_ref, wt_ref, c_ref, inc_ref,
+                 e_ref, s_ref, g_ref, d_ref, gm_ref, gs_ref, wm_ref, ws_ref, p0, s0, y0, p1, s1, y1, g1_ref,
+                 x_ref, m_ref, *rest):
+    members, levels, rows, cols = ens_ref.shape
+    dims = dict(members=members, levels=levels, rows=rows, cols=cols)
+    ens_bufs, first_bufs, second_bufs, work, sum_bufs = rest[:9], rest[9:15], rest[15:21], rest[21:27], rest[27:]
+    prep_kernel(ens_ref, cell_ref, level_ref, inn_ref, wt_ref, e_ref, s_ref, g_ref, d_ref, gm_ref, gs_ref,
+                wm_ref, ws_ref, *ens_bufs, *first_bufs)
+    g_kernel(e_ref, s_ref, gm_ref, gs_ref, wm_ref, ws_ref, p0, s0, y0, *work, **dims)
+    next_kernel(y0, d_ref, gm_ref, gs_ref, g1_ref, *second_bufs)
+    g_kernel(e_ref, s_ref, gm_ref, gs_ref, wm_ref, ws_ref, p1, s1, y1, *work, **dims)
+    x_ref[...] = jnp.zeros_like(x_ref)
+    for k, (a, b) in enumerate(((g_ref, y0), (g1_ref, y0), (g1_ref, y1), (None, y1))):
+        v = d_ref[...] * y1[...] * y1[...] if a is None else a[...] * b[...]
+        x_ref[k:k + 1, :] = jnp.sum(v.reshape(levels * rows, cols), axis=0, keepdims=True)
+    sum_kernel(x_ref, m_ref, *sum_bufs)
+    out_kernel(m_ref, p0, s0, p1, s1, y0, y1, c_ref, inc_ref)
+
+
+def on_device(ensemble, obs_cell, obs_level, innovation, obs_weight):
+    members, levels, rows, cols = ensemble.shape
+    hr = rows + 2 * W
+    f = members * levels
+    groups = members // 8
+    pairs = groups // 2
+    count = groups + pairs
+    q = levels * pairs
     nx, ny = lax.axis_size("gx"), lax.axis_size("gy")
+    f32 = jnp.float32
     vm = pl.BlockSpec(memory_space=pltpu.VMEM)
     dma = pltpu.SemaphoreType.DMA
-    return pl.pallas_call(
-        sum_kernel,
-        out_shape=jax.ShapeDtypeStruct(x.shape, x.dtype),
-        in_specs=[vm],
-        out_specs=vm,
-        scratch_shapes=[pltpu.VMEM(x.shape, x.dtype), pltpu.VMEM((nx - 1,) + x.shape, x.dtype),
-                        pltpu.VMEM((ny - 1,) + x.shape, x.dtype),
-                        dma((nx - 1,)), dma((nx - 1,)), dma((ny - 1,)), dma((ny - 1,))],
-        compiler_params=pltpu.CompilerParams(collective_id=0, has_side_effects=True),
-    )(x)
-
-
-def on_device(ensemble, obs_cell, obs_level, innovation, obs_weight):
-    members, levels, rows, cols = ensemble.shape
-    f32 = jnp.float32
-    vm = pl.BlockSpec(memory_space=pltpu.VMEM)
+    v = lambda *s: pltpu.VMEM(s, f32)
     flat = lambda a: a.reshape(1, -1)
-    e2, s2, g0, dd, gm, gs = prep(ensemble, flat(obs_cell), flat(obs_level), flat(innovation), flat(obs_weight))
-    wm, ws = pl.pallas_call(
-        functools.partial(weight_kernel, cols=cols),
-        out_shape=(jax.ShapeDtypeStruct((2 * cols, SWEEPS * cols), jnp.bfloat16),) * 2,
+    image = [v(levels * groups, hr, 8, cols), v(levels * pairs, hr, 8, cols), v(levels, rows, cols)]
+    weights = [pltpu.VMEM((2 * cols, SWEEPS * cols), jnp.bfloat16)] * 2
+    control, increment = pl.pallas_call(
+        whole_kernel,
+        out_shape=(jax.ShapeDtypeStruct((f * rows, cols), f32), jax.ShapeDtypeStruct((levels, rows, cols), f32)),
+        in_specs=[vm] * 5,
         out_specs=(vm, vm),
-    )()
-    p0, ps0, y0 = g_apply(e2, s2, gm, gs, wm, ws, ensemble.shape)
-    gm1, gs1 = next_state(y0, dd)
-    p1, ps1, y1 = g_apply(e2, s2, gm1, gs1, wm, ws, ensemble.shape)
-    sums = jnp.stack([jnp.sum(v, axis=(0, 1)) for v in (g0 * y0, dd * y0 * y0, dd * y0 * y1, dd * y1 * y1)])
-    m = sum_all(jnp.concatenate([sums, jnp.zeros_like(sums)]))
-    control, increment = pl.pallas_call(
-        out_kernel,
-        out_shape=(jax.ShapeDtypeStruct((members * levels * rows, cols), f32), jax.ShapeDtypeStruct((levels, rows, cols), f32)),
-        in_specs=[vm] * 7,
-        out_specs=(vm, vm),
-        compiler_params=pltpu.CompilerParams(vmem_limit_bytes=60000000),
-    )(m, p0, ps0, p1, ps1, y0, y1)
+        scratch_shapes=[v(f * hr, cols), v(q * 8 * hr, cols), v(levels, rows, cols), v(levels, rows, cols),
+                        v(levels, hr, cols), v(levels, hr, cols)] + weights + image + image
+        + [v(levels, rows, cols), v(8, cols), v(8, cols)]
+        + [v(f, rows, cols), v(q, rows, cols), v(q, rows, cols), v(2, f, W, cols), v(q, rows, cols), v(q, rows, cols),
+           v(4, q, W, cols), dma((8,)), dma((8,))]
+        + state_scratch(levels, cols) + state_scratch(levels, cols)
+        + [v(hr, cols), v(levels, hr, 8, cols), v(levels, hr, 8, cols), v(count, hr, 8, cols),
+           pltpu.VMEM((count, hr * 8, 2 * cols), jnp.bfloat16), v(count, hr * 8, SWEEPS * cols)]
+        + [v(8, cols), v(nx - 1, 8, cols), v(ny - 1, 8, cols), dma((nx - 1,)), dma((nx - 1,)), dma((ny - 1,)), dma((ny - 1,))],
+        compiler_params=pltpu.CompilerParams(collective_id=0, has_side_effects=True, vmem_limit_bytes=64000000),
+    )(ensemble, flat(obs_cell), flat(obs_level), flat(innovation), flat(obs_weight))
     return (control.reshape(members, levels, rows, cols), increment)
 
 

time: 106 us -> 81.2 us (0.77)
  Pallas kernels: 104 us -> 76.6 us
  local copies, waits for them, and re-layouts: 0.62 us -> 3.82 us
    pallas_call x7 -> x1, Pallas kernels: 104 us -> 76.6 us  [on_device(): pl.pallas_call(whole_kernel, out_shape=(jax.ShapeDtypeStruct((f * rows, c...]
    unnamed x6 -> x4, local copies, waits for them, and re-layouts: 0.01 us -> 3.82 us
where the time goes in v4:
time: 81.2 us; the launch traced here: 81.1 us
  Pallas kernels  76.6 us (94%)
  local copies, waits for them, and re-layouts  3.82 us (5%)
    pallas_call x1, Pallas kernels, on_device(): pl.pallas_call(whole_kernel, out_shape=(jax.ShapeDtypeStruct((f * rows, c...  76.6 us
    unnamed x4, local copies, waits for them, and re-layouts  3.82 us

profile of v4, /device:TPU:0, one launch (start us, length us, event | category | flops | bytes accessed | tf_op | source)
XLA Modules:
  0.0 81.1 jit_solution(14068196049407560372)
XLA Ops:
  0.6 76.6 %shard_map.68 = (f32[4096,128]{1,0:T(8,128)}, f32[2,64,128]{2,1,0:T(8,128)}) custom-call(bf16[32,2,64,128]{3,2,1,0:T(8,128)(2,1)} %ens_ref.1, s32[1,2048]{1,0:T(1,128)} %bitcast.6, s32[1,2048]{1,0:T(1,128)} %bitcast.7, f32[1,2048]{1,0:T(1,128)} %bitcast.8, f32[1,2048]{1,0:T(1,128)} %bitcast.9), custom_call_target="tpu_custom_call" | custom-call | tf_op jit(solution)/shard_map/pallas_call | solution.py:473
  77.2 0.0 copy-start
  77.2 3.2 %copy.9 = f32[32,2,64,128]{3,2,1,0:T(8,128)} copy(f32[32,2,64,128]{3,2,1,0:T(8,128)} %bitcast.5) | data formatting | bytes 4194304
  80.4 0.0 copy-done
  80.4 0.6 copy.10
Async XLA Ops:
  77.2 3.2 %copy-start = (f32[2,64,128]{2,1,0:T(8,128)S(1)}, f32[2,64,128]{2,1,0:T(8,128)}, u32[]{:S(2)}) copy-start(f32[2,64,128]{2,1,0:T(8,128)} %get-tuple-element.9) | copy-start | bytes 196612
